TPU v7x, 256 devices: a whole 4x4x8 slice. The times are simulated.
256 devices in a mesh: ep: 32 (over x, z), tp: 8 (over y, core).
Axes of the slice: x: 4, y: 4, z: 8, core: 2. Of those that a mesh axis runs over, the one named last changes fastest.
Arguments:
- tokens: bfloat16 [4096, 3072], P('ep', 'tp'), may hold values from -6 to 6
- expert_ids: int32 [4096, 2], P('ep'), may hold values from 0 to 7, all different within a row
- route_share: float32 [4096], P('ep'), may hold values from 0.5 to 0.95
- w_gate: bfloat16 [65536, 3072], P(('ep', 'tp')), may hold values from -0.109375 to 0.109375
- w_up: bfloat16 [65536, 3072], P(('ep', 'tp')), may hold values from -0.109375 to 0.109375
- w_down: bfloat16 [65536, 3072], P(('ep', 'tp')), may hold values from -0.0625 to 0.0625
- reward_head: float32 [3072], P('tp'), may hold values from -0.109375 to 0.109375
- upstream: bfloat16 [4096, 3072], P('ep', 'tp'), may hold values from -4 to 4
- pair_order: int32 [64], replicated, may hold values from 0 to 63, each once
Outputs:
- layer_out: bfloat16 [4096, 3072], P('ep', 'tp')
- rewards: float32 [64], replicated
- pair_loss: float32 [], replicated
- grad_tokens: bfloat16 [4096, 3072], P('ep', 'tp')
- grad_gate: bfloat16 [65536, 3072], P(('ep', 'tp'))
- grad_up: bfloat16 [65536, 3072], P(('ep', 'tp'))
- grad_down: bfloat16 [65536, 3072], P(('ep', 'tp'))
Inputs may be any that keep to these rules, and one draw needn't show every extreme that they name: `expert_ids`: each row names 2 different experts. `pair_order`: each of the 64 sequence indices appears once.
All inputs are finite; a program needn't handle non-finite values.
Results may differ from a plain program's by a relative error of at most 0.014.
Values may be sent and summed in bfloat16 or wider, within the bound.
No kernel may reach another device: no remote copies, remote signals or barrier semaphores. Data moves between devices by JAX's collectives and lax.ppermute only.
A program may use at most 128 MiB of HBM per device.

v0:
```python
import math

import jax
import jax.numpy as jnp
from jax import lax
from jax.experimental import pallas as pl
from jax.experimental.pallas import tpu as pltpu
from jax.sharding import Mesh
from jax.sharding import PartitionSpec as P


EXPERTS = 8
SEQ_LEN = 64
EP = ("ep_x", "ep_z")
TP = ("tp_y", "tp_c")
EP_TP = EP + TP


loss_scale = 256.0
VMEM_MIB = 60
bf16, f32 = jnp.bfloat16, jnp.float32


def route_kernel(at_ref, ids_ref, share_ref, tokens_ref, upstream_ref, *refs):
    mine_ref, theirs_ref, meta_ref, picker_ref, mixing_ref, both, meta = refs
    slots, count = picker_ref.shape
    local_width = tokens_ref.shape[1]
    half_cap = slots // (2 * EXPERTS)
    lane = lax.broadcasted_iota(jnp.int32, (count, count), 1)
    row = lax.broadcasted_iota(jnp.int32, (count, count), 0)
    earlier = (row < lane).astype(f32).astype(bf16)
    expert = lax.broadcasted_iota(jnp.int32, (2 * EXPERTS, count), 0)
    hot = [(expert == ids_ref[pl.ds(i, 1)]).astype(f32) for i in (0, 1)]
    before = [plain(h.astype(bf16), earlier) for h in hot]
    before[1] = before[1] + jnp.sum(hot[0], axis=1, keepdims=True)
    slot_iota = lax.broadcasted_iota(jnp.int32, (slots, count), 0)
    share = share_ref[...]
    picker = jnp.zeros((slots, count), f32)
    shares = jnp.zeros((slots, count), f32)
    for i, weight in ((0, share), (1, 1.0 - share)):
        rank = jnp.sum(before[i] * hot[i], axis=0, keepdims=True).astype(jnp.int32)
        late = (rank >= half_cap).astype(jnp.int32)
        slot = late * (slots // 2 - half_cap) + ids_ref[pl.ds(i, 1)] * half_cap + rank
        slot = jnp.where(rank < 2 * half_cap, slot, -1)
        match = (slot_iota == slot).astype(f32)
        picker = picker + match
        shares = shares + match * weight
    by_slot = picker.astype(bf16)
    picker_ref[...] = by_slot
    mixing_ref[...] = shares
    slot_share = jnp.sum(shares, axis=1, keepdims=True)
    both[:, pl.ds(0, local_width)] = plain(by_slot, tokens_ref[...]).astype(bf16)
    both[:, pl.ds(local_width, local_width)] = (
        plain(by_slot, upstream_ref[...]) * slot_share
    ).astype(bf16)
    lane = lax.broadcasted_iota(jnp.int32, (slots, count), 1)
    table = jnp.zeros((slots, count), f32)
    for seq in range(count // SEQ_LEN):
        part = jnp.where(lane // SEQ_LEN == seq, shares, 0.0)
        part = jnp.sum(part, axis=1, keepdims=True)
        high = part.astype(bf16).astype(f32)
        table = jnp.where(lane == 2 * seq, high, table)
        table = jnp.where(lane == 2 * seq + 1, part - high, table)
    meta[...] = table.astype(bf16)
    half = slots // 2
    core = at_ref[1]
    own = pl.ds(pl.multiple_of(core * half, half), half)
    other = pl.ds(pl.multiple_of((1 - core) * half, half), half)
    mine_ref[...] = both[own]
    theirs_ref[...] = both[other]
    meta_ref[...] = meta[own]


def pack_kernel(at_ref, mine_ref, got_ref, *refs):
    out_ref = refs[-1]
    start = 0 if len(refs) == 1 else mine_ref.shape[1] // 2
    local_width = mine_ref.shape[1] // 2
    half_cap = mine_ref.shape[0] // EXPERTS
    replicas = out_ref.shape[0] // mine_ref.shape[0]
    columns = pl.ds(start, local_width)
    for core in (0, 1):
        low, high = (mine_ref, got_ref) if core == 0 else (got_ref, mine_ref)

        @pl.when(at_ref[1] == core)
        def _(low=low, high=high):
            for i in range(EXPERTS * replicas):
                src = pl.ds(i // replicas * half_cap, half_cap)
                dst = pl.ds(i * half_cap, half_cap)
                out_ref[dst, pl.ds(0, local_width)] = low[src, columns]
                out_ref[dst, pl.ds(local_width, local_width)] = high[src, columns]
                for meta_ref in refs[:-1]:
                    out_ref[dst, pl.ds(2 * local_width, 128)] = meta_ref[src]


def rot(value, shift):
    return lax.ppermute(value, "tp_y", [(i, (i + shift) % 4) for i in range(4)])


def swap(value):
    return lax.ppermute(value, "tp_c", [(0, 1), (1, 0)])


def exchange(blocks):
    arrived = lax.all_to_all(
        blocks.transpose(1, 0, 2), EP, split_axis=1, concat_axis=1, tiled=True
    )
    return arrived.transpose(1, 0, 2)


def gather_features(rows):
    half = rows.shape[0] // 2
    back, ahead = rot(rows, 1), rot(rows, -1)
    far_low, far_high = rot(back[:half], 1), rot(ahead[half:], -1)
    return (rows, ahead, far_low, far_high, back)


def add(*terms):
    return sum((t.astype(f32) for t in terms[1:]), terms[0].astype(f32)).astype(bf16)


def scatter_start(pieces):
    own, ahead, far_low, far_high, back = pieces
    half = far_low.shape[0]
    via_low, via_high = rot(far_low, 1), rot(far_high, -1)
    onward = add(ahead, jnp.pad(via_low, ((0, half), (0, 0))))
    backward = add(back, jnp.pad(via_high, ((half, 0), (0, 0))))
    return own, rot(onward, 1), rot(backward, -1)


def piece_halves(refs):
    own, ahead, far_low, far_high, back = refs
    half = far_low.shape[0]
    low, high = pl.ds(0, half), pl.ds(half, half)
    return (
        (own.at[low], own.at[high]),
        (ahead.at[low], ahead.at[high]),
        (far_low, far_high),
        (back.at[low], back.at[high]),
    )


def load_piece(step, refs, rows):
    half = rows.shape[0] // 2
    for k, (low, high) in enumerate(piece_halves(refs)):

        @pl.when(step == k)
        def _(low=low, high=high):
            rows[pl.ds(0, half)] = low[...]
            rows[pl.ds(half, half)] = high[...]


def cross(a, b):
    return lax.dot_general(a, b, (((1,), (1,)), ((), ())), preferred_element_type=f32)


def across(a, b):
    return lax.dot_general(a, b, (((0,), (0,)), ((), ())), preferred_element_type=f32)


def plain(a, b):
    return lax.dot_general(a, b, (((1,), (0,)), ((), ())), preferred_element_type=f32)


def near_kernel(y_ref, *refs):
    x_refs = refs[:3]
    weights, accs, rows = refs[3:7], refs[7:9], refs[9]
    width = weights[0].shape[0]
    step = pl.program_id(0)

    @pl.when(step == 0)
    def _():
        for acc in accs:
            acc[...] = jnp.zeros_like(acc)

    for k, ref in enumerate(x_refs):

        @pl.when(step == k)
        def _(ref=ref):
            rows[...] = ref[...]

    chunk = rows.shape[0] // 2

    @pl.loop(0, 2)
    def _(i):
        at = pl.ds(pl.multiple_of(i * chunk, chunk), chunk)
        for j, weight in enumerate(weights):
            accs[j // 2][at, pl.ds(j % 2 * width, width)] += cross(rows[at], weight[...])


def fwd_kernel(y_ref, *refs):
    far_refs = refs[:2]
    wg0, wg1, wu0, wu1, rh_ref, meta_ref, gate_ref, up_ref = refs[2:10]
    slope_ref, silu_ref, hidden_ref, score_ref = refs[10:14]
    gate_acc, up_acc, rows = refs[14:]
    half, width = rows.shape[0] // 2, wg0.shape[0]
    left, right = pl.ds(0, width), pl.ds(width, width)
    rows[pl.ds(0, half)] = far_refs[0][...]
    rows[pl.ds(half, half)] = far_refs[1][...]
    gate_acc[:, left] = gate_ref[:, left] + cross(rows[...], wg0[...])
    gate_acc[:, right] = gate_ref[:, right] + cross(rows[...], wg1[...])
    up_acc[:, left] = up_ref[:, left] + cross(rows[...], wu0[...])
    up_acc[:, right] = up_ref[:, right] + cross(rows[...], wu1[...])
    finish_forward(
        rh_ref, meta_ref, slope_ref, silu_ref, hidden_ref, score_ref, gate_acc, up_acc
    )


def finish_forward(
    rh_ref, meta_ref, slope_ref, silu_ref, hidden_ref, score_ref, gate_acc, up_acc
):
    chunk = gate_acc.shape[0] // 8

    @pl.loop(0, 8)
    def _(i):
        at = pl.ds(pl.multiple_of(i * chunk, chunk), chunk)
        gate, up = gate_acc[at], up_acc[at]
        sig = jax.nn.sigmoid(gate)
        silu = gate * sig
        hidden = (silu * up).astype(bf16)
        silu_ref[at] = silu
        slope_ref[at] = up * (sig * (1.0 + gate * (1.0 - sig)))
        hidden_ref[at] = hidden
        score = jnp.sum(hidden.astype(f32) * rh_ref[...], axis=1, keepdims=True)
        gate_acc[at, pl.ds(0, 128)] = score * meta_ref[at].astype(f32)

    scores = gate_acc[:, pl.ds(0, 128)].reshape(score_ref.shape[0], -1, 128)
    scores = jnp.sum(scores, axis=1)
    lane = lax.broadcasted_iota(jnp.int32, scores.shape, 1)
    first = jnp.sum(jnp.where(lane < 2, scores, 0.0), axis=1, keepdims=True)
    second = jnp.sum(jnp.where(lane < 2, 0.0, scores), axis=1, keepdims=True)
    score_ref[...] = jnp.where(lane == 0, first, second)


def down_kernel(y_ref, hidden_ref, wd0, wd1, low_ref, high_ref):
    width, half = wd0.shape[0], low_ref.shape[0]
    left, right = pl.ds(0, width), pl.ds(width, width)
    for i, ref in enumerate((low_ref, high_ref)):
        at = pl.ds(i * half, half)
        ref[...] = (
            plain(hidden_ref[at, left], wd0[...]) + plain(hidden_ref[at, right], wd1[...])
        ).astype(bf16)


def side_kernel(y_ref, hidden_ref, wd0, wd1, *refs):
    out_refs, rows = refs[:3], refs[3]
    width = wd0.shape[0]
    left, right = pl.ds(0, width), pl.ds(width, width)
    chunk = rows.shape[0] // 2

    @pl.loop(0, 2)
    def _(i):
        at = pl.ds(pl.multiple_of(i * chunk, chunk), chunk)
        rows[at] = (
            plain(hidden_ref[at, left], wd0[...]) + plain(hidden_ref[at, right], wd1[...])
        ).astype(bf16)

    for k, ref in enumerate(out_refs):

        @pl.when(pl.program_id(0) == k)
        def _(ref=ref):
            ref[...] = rows[...]


def back_kernel(y_ref, *refs):
    u_refs, (wd0, wd1, out_ref, rows) = refs[:5], refs[5:]
    width = wd0.shape[0]
    left, right = pl.ds(0, width), pl.ds(width, width)
    step = pl.program_id(0)

    @pl.when(step == 0)
    def _():
        out_ref[...] = jnp.zeros_like(out_ref)

    load_piece(step, u_refs, rows)
    out_ref[:, left] += cross(rows[...], wd0[...])
    out_ref[:, right] += cross(rows[...], wd1[...])


def bwd_kernel(y_ref, *refs):
    wg0, wg1, wu0, wu1, rh_ref, meta_ref, seq_ref, partial_ref, slope_ref, silu_ref = refs[:10]
    gate_grad_ref, up_grad_ref, coef_ref, low_ref, high_ref = refs[10:15]
    width, half = wg0.shape[0], low_ref.shape[0]
    left, right = pl.ds(0, width), pl.ds(width, width)
    count = partial_ref.shape[0]
    blocks = seq_ref.shape[0]
    lane = lax.broadcasted_iota(jnp.int32, (blocks, 128), 1)
    first = jnp.broadcast_to(seq_ref[:, pl.ds(0, 1)], lane.shape)
    second = jnp.broadcast_to(seq_ref[:, pl.ds(1, 1)], lane.shape)
    by_lane = jnp.where(lane < 2, first, jnp.where(lane < 4, second, 0.0))
    shares = meta_ref[...].astype(f32).reshape(blocks, count // blocks, 128)
    terms = (shares * by_lane[:, None, :]).reshape(count, 128)
    coef_ref[...] = jnp.sum(terms, axis=1, keepdims=True)
    chunk = count // 8

    @pl.loop(0, 8)
    def _(i):
        at = pl.ds(pl.multiple_of(i * chunk, chunk), chunk)
        hidden_grad = partial_ref[at] + coef_ref[at] * rh_ref[...]
        gate_grad_ref[at] = (hidden_grad * slope_ref[at]).astype(bf16)
        up_grad_ref[at] = (hidden_grad * silu_ref[at]).astype(bf16)

    for i, ref in enumerate((low_ref, high_ref)):
        at = pl.ds(i * half, half)
        ref[...] = (
            plain(gate_grad_ref[at, left], wg0[...])
            + plain(gate_grad_ref[at, right], wg1[...])
            + plain(up_grad_ref[at, left], wu0[...])
            + plain(up_grad_ref[at, right], wu1[...])
        ).astype(bf16)


def rest_kernel(y_ref, *refs):
    wg0, wg1, wu0, wu1, gate_grad_ref, up_grad_ref = refs[:6]
    out_refs, rows = refs[6:9], refs[9]
    width = wg0.shape[0]
    left, right = pl.ds(0, width), pl.ds(width, width)
    chunk = rows.shape[0] // 2

    @pl.loop(0, 2)
    def _(i):
        at = pl.ds(pl.multiple_of(i * chunk, chunk), chunk)
        rows[at] = (
            plain(gate_grad_ref[at, left], wg0[...])
            + plain(gate_grad_ref[at, right], wg1[...])
            + plain(up_grad_ref[at, left], wu0[...])
            + plain(up_grad_ref[at, right], wu1[...])
        ).astype(bf16)

    for k, ref in enumerate(out_refs):

        @pl.when(pl.program_id(0) == k)
        def _(ref=ref):
            ref[...] = rows[...]


def grad_kernel(y_ref, *refs):
    x_refs, u_refs = refs[:5], refs[5:10]
    hidden_ref, gate_grad_ref, up_grad_ref, coef_ref, rh_ref = refs[10:15]
    own_ref, other_ref, left, rows = refs[15:]
    width = left.shape[1]
    step = pl.program_id(0)

    @pl.when(step == 0)
    def _():
        for i, ref in enumerate((gate_grad_ref, up_grad_ref, hidden_ref)):
            turned = ref[...].T
            left[2 * i] = turned[:width]
            left[2 * i + 1] = turned[width:]

    load_piece(step, x_refs, rows.at[0])
    load_piece(step, u_refs, rows.at[1])
    rows[1] = (rows[1].astype(f32) + coef_ref[...] * rh_ref[...]).astype(bf16)

    @pl.loop(0, 3)
    def _(i):
        at = pl.ds(pl.multiple_of(i * width, width), width)
        own_ref[at] = plain(left[2 * i], rows[i // 2]).astype(bf16)
        other_ref[at] = plain(left[2 * i + 1], rows[i // 2]).astype(bf16)


def whole(shape):
    return pl.BlockSpec(shape, lambda k, y: (0,) * len(shape))


def columns(width, block):
    return pl.BlockSpec((width, block), lambda k, y: (0, (y[0] + k) % 4))


def near_columns(width, block):
    return pl.BlockSpec((width, block), lambda k, y: (0, (y[0] + k + k // 2) % 4))


def far_columns(width, block):
    return pl.BlockSpec((width, block), lambda k, y: (0, (y[0] + 2) % 4))


def piece_specs(rows, block):
    full, part = whole((rows, block)), whole((rows // 2, block))
    return [full, full, part, part, full]


def call(kernel, steps, in_specs, out_specs, out_shape, scratch, flops, args):
    return pl.pallas_call(
        kernel,
        grid_spec=pltpu.PrefetchScalarGridSpec(
            num_scalar_prefetch=1,
            grid=(steps,),
            in_specs=in_specs,
            out_specs=out_specs,
            scratch_shapes=scratch,
        ),
        out_shape=out_shape,
        compiler_params=pltpu.CompilerParams(
            dimension_semantics=("arbitrary",), vmem_limit_bytes=VMEM_MIB * 1024 * 1024
        ),
        cost_estimate=pl.CostEstimate(flops=flops, bytes_accessed=20_000_000, transcendentals=0),
    )(*args)


def layer(
    tokens, expert_ids, route_share, w_gate, w_up, w_down, reward_head, upstream, pair_order
):
    tok_count, local_width = tokens.shape
    capacity = tok_count * expert_ids.shape[1] // EXPERTS
    ep_size = lax.axis_size(EP)
    replicas = ep_size // EXPERTS
    half_cap = capacity // 2
    block = 2 * local_width
    rows = ep_size * half_cap
    hid = w_gate.shape[0]
    core = lax.axis_index("tp_c")
    place = jnp.stack([lax.axis_index("tp_y"), core]).astype(jnp.int32)

    wg_other, wu_other, wd_other = swap(w_gate), swap(w_up), swap(w_down)

    seq_local = tok_count // SEQ_LEN
    half_slots = EXPERTS * half_cap
    half_rows = jax.ShapeDtypeStruct((half_slots, block), bf16)
    mine, theirs, meta, picker, mixing = call(
        route_kernel,
        1,
        [whole((2, tok_count)), whole((1, tok_count))] + [whole((tok_count, local_width))] * 2,
        [whole((half_slots, block))] * 2
        + [whole((half_slots, 128))]
        + [whole((2 * half_slots, tok_count))] * 2,
        [
            half_rows,
            half_rows,
            jax.ShapeDtypeStruct((half_slots, 128), bf16),
            jax.ShapeDtypeStruct((2 * half_slots, tok_count), bf16),
            jax.ShapeDtypeStruct((2 * half_slots, tok_count), f32),
        ],
        [
            pltpu.VMEM((2 * half_slots, block), bf16),
            pltpu.VMEM((2 * half_slots, 128), bf16),
        ],
        1_000_000,
        (place, expert_ids.T, route_share[None, :], tokens, upstream),
    )
    theirs = swap(theirs)
    half_spec = whole((half_slots, block))
    token_block = call(
        pack_kernel,
        1,
        [half_spec] * 2,
        whole((rows, block)),
        jax.ShapeDtypeStruct((rows, block), bf16),
        [],
        1_000_000,
        (place, mine, theirs),
    )
    grad_block = call(
        pack_kernel,
        1,
        [half_spec] * 2 + [whole((half_slots, 128))],
        whole((rows, block + 128)),
        jax.ShapeDtypeStruct((rows, block + 128), bf16),
        [],
        1_000_000,
        (place, mine, theirs, meta),
    )

    def to_experts(block_rows):
        width = block_rows.shape[1]
        return exchange(block_rows.reshape(ep_size, half_cap, width)).reshape(rows, width)

    token_rows = to_experts(token_block)
    grad_full = to_experts(grad_block)

    head = lax.all_gather(reward_head, TP, axis=0, tiled=True)
    head_own = jnp.sum(w_down.astype(f32) * head[None, :], axis=1)
    head_other = jnp.sum(wd_other.astype(f32) * head[None, :], axis=1)
    head_row = jnp.concatenate([head_own, head_other])[None, :]
    local_scores = jnp.sum(tokens.astype(f32) * reward_head[None, :], axis=1)
    local_rewards = jnp.sum(local_scores.reshape(seq_local, SEQ_LEN), axis=1)
    seq_total = pair_order.shape[0]
    offset = lax.axis_index(EP) * seq_local
    placed = lax.dynamic_update_slice(jnp.zeros((seq_total,), f32), local_rewards, (offset,))
    token_rows, head_row, placed = lax.optimization_barrier((token_rows, head_row, placed))

    token_pieces = gather_features(token_rows)
    grad_pieces = gather_features(grad_full[:, :block])

    slots_hid = (rows, 2 * hid)
    meta_spec = pl.BlockSpec((rows, 128), lambda k, y: (0, block // 128))
    work = rows * 2 * hid * 4 * block
    own_rows, ahead_rows, far_low, far_high, back_rows = token_pieces
    gate_weights = (w_gate, wg_other, w_up, wu_other)
    full, part = whole((rows, block)), whole((rows // 2, block))
    gate, up = call(
        near_kernel,
        3,
        [full] * 3 + [near_columns(hid, block)] * 4,
        [whole(slots_hid)] * 2,
        [jax.ShapeDtypeStruct(slots_hid, f32)] * 2,
        [pltpu.VMEM((rows, block), bf16)],
        3 * work,
        (place, own_rows, ahead_rows, back_rows, *gate_weights),
    )
    slope, silu, hidden, score = call(
        fwd_kernel,
        1,
        [part] * 2
        + [far_columns(hid, block)] * 4
        + [whole((1, 2 * hid)), meta_spec]
        + [whole(slots_hid)] * 2,
        [whole(slots_hid)] * 3 + [whole((ep_size, 128))],
        [jax.ShapeDtypeStruct(slots_hid, f32)] * 2
        + [jax.ShapeDtypeStruct(slots_hid, bf16), jax.ShapeDtypeStruct((ep_size, 128), f32)],
        [pltpu.VMEM(slots_hid, f32)] * 2 + [pltpu.VMEM((rows, block), bf16)],
        work,
        (place, far_low, far_high, *gate_weights, head_row, grad_full, gate, up),
    )
    placed = (placed + score[:, :seq_local].reshape(seq_total)).reshape(2, 1, seq_total // 2)
    everyone = lax.axis_size(EP_TP)
    spread = jnp.broadcast_to(placed, (2, everyone, seq_total // 2))
    spread = lax.all_to_all(spread, EP_TP, split_axis=1, concat_axis=1, tiled=True)
    rewards = jnp.sum(spread, axis=1).reshape(seq_total) / math.sqrt(SEQ_LEN)

    half_shape = jax.ShapeDtypeStruct((rows // 2, block), bf16)
    full_shape = jax.ShapeDtypeStruct((rows, block), bf16)
    down_low, down_high = call(
        down_kernel,
        1,
        [whole(slots_hid)] + [far_columns(hid, block)] * 2,
        [part] * 2,
        [half_shape] * 2,
        [],
        work // 2,
        (place, hidden, w_down, wd_other),
    )
    down_own, down_ahead, down_back = call(
        side_kernel,
        3,
        [whole(slots_hid)] + [near_columns(hid, block)] * 2,
        [full] * 3,
        [full_shape] * 3,
        [pltpu.VMEM((rows, block), bf16)],
        3 * work // 2,
        (place, hidden, w_down, wd_other),
    )
    down_pieces = (down_own, down_ahead, down_low, down_high, down_back)
    partial = call(
        back_kernel,
        4,
        piece_specs(rows, block) + [columns(hid, block)] * 2,
        [whole(slots_hid)],
        [jax.ShapeDtypeStruct(slots_hid, f32)],
        [pltpu.VMEM((rows, block), bf16)],
        2 * work,
        (place, *grad_pieces, w_down, wd_other),
    )[0]
    down_sums = scatter_start(down_pieces)

    seq_iota = jnp.arange(seq_total, dtype=jnp.int32)
    chosen_hot = (pair_order[0::2][:, None] == seq_iota[None, :]).astype(f32)
    rejected_hot = (pair_order[1::2][:, None] == seq_iota[None, :]).astype(f32)
    margin = jnp.sum((chosen_hot - rejected_hot) * rewards[None, :], axis=1)
    pair_loss = jnp.mean(jax.nn.softplus(-margin))
    pair_weight = jax.nn.sigmoid(-margin)
    seq_coef = jnp.sum(pair_weight[:, None] * (rejected_hot - chosen_hot), axis=0)
    token_coef = jnp.repeat(lax.dynamic_slice_in_dim(seq_coef, offset, seq_local), SEQ_LEN)
    grad_out = (
        upstream.astype(f32)
        + loss_scale * token_coef[:, None] * reward_head[None, :] / math.sqrt(SEQ_LEN)
    ).astype(bf16)
    scaled = (seq_coef * (loss_scale / math.sqrt(SEQ_LEN))).reshape(ep_size, seq_local)

    gate_grad, up_grad, slot_coef, far_low, far_high = call(
        bwd_kernel,
        1,
        [far_columns(hid, block)] * 4
        + [whole((1, 2 * hid)), meta_spec, whole((ep_size, seq_local))]
        + [whole(slots_hid)] * 3,
        [whole(slots_hid)] * 2 + [whole((rows, 1))] + [part] * 2,
        [jax.ShapeDtypeStruct(slots_hid, bf16)] * 2
        + [jax.ShapeDtypeStruct((rows, 1), f32)]
        + [jax.ShapeDtypeStruct((rows // 2, block), bf16)] * 2,
        [],
        work,
        (place, *gate_weights, head_row, grad_full, scaled, partial, slope, silu),
    )
    own_sums, ahead_sums, back_sums = call(
        rest_kernel,
        3,
        [near_columns(hid, block)] * 4 + [whole(slots_hid)] * 2,
        [full] * 3,
        [jax.ShapeDtypeStruct((rows, block), bf16)] * 3,
        [pltpu.VMEM((rows, block), bf16)],
        3 * work,
        (place, *gate_weights, gate_grad, up_grad),
    )
    input_sums = scatter_start((own_sums, ahead_sums, far_low, far_high, back_sums))

    own_grads, other_grads = call(
        grad_kernel,
        4,
        piece_specs(rows, block) * 2
        + [whole(slots_hid)] * 3
        + [whole((rows, 1)), columns(1, block)],
        [columns(3 * hid, block)] * 2,
        [jax.ShapeDtypeStruct((3 * hid, 4 * block), bf16)] * 2,
        [pltpu.VMEM((6, hid, rows), bf16), pltpu.VMEM((2, rows, block), bf16)],
        6 * work,
        (place, *token_pieces, *grad_pieces, hidden, gate_grad, up_grad, slot_coef, head[None, :]),
    )
    other_grads = swap(other_grads)
    grad_gate, grad_up, grad_down = (
        add(own_grads[i * hid : (i + 1) * hid], other_grads[i * hid : (i + 1) * hid])
        for i in range(3)
    )

    def come_back(pieces):
        summed = add(*pieces).reshape(ep_size, half_cap, block)
        arrived = exchange(summed).astype(f32)
        sums = jnp.sum(arrived.reshape(EXPERTS, replicas, half_cap, block), axis=1)
        sums = sums.astype(bf16).reshape(EXPERTS * half_cap, block)
        left, right = sums[:, :local_width], sums[:, local_width:]
        mine = jnp.where(core == 0, left, right)
        theirs = swap(jnp.where(core == 0, right, left))
        return jnp.concatenate(
            [jnp.where(core == 0, mine, theirs), jnp.where(core == 0, theirs, mine)], axis=0
        )

    mixed_sum = across(mixing, come_back(down_sums).astype(f32))
    layer_out = (tokens.astype(f32) + mixed_sum).astype(bf16)
    returned = across(picker, come_back(input_sums))
    grad_tokens = (grad_out.astype(f32) + returned).astype(bf16)
    return (layer_out, rewards, pair_loss, grad_tokens, grad_gate, grad_up, grad_down)


def solution(mesh):
    split = Mesh(mesh.devices.reshape(4, 8, 4, 2), EP_TP)
    in_specs = (
        P(EP, TP),
        P(EP, None),
        P(EP),
        P(EP_TP, None),
        P(EP_TP, None),
        P(EP_TP, None),
        P(TP),
        P(EP, TP),
        P(),
    )
    out_specs = (P(EP, TP), P(), P(), P(EP, TP), P(EP_TP, None), P(EP_TP, None), P(EP_TP, None))
    return jax.shard_map(layer, mesh=split, in_specs=in_specs, out_specs=out_specs, check_vma=False)
```

profile of v0, /device:TPU:32, one launch (start us, length us, event | category | flops | bytes accessed | tf_op | source)
XLA Modules:
  0.0 275.0 jit_solution(11310390251713469231)
XLA Ops:
  1.3 2.8 %shard_map.144 = (bf16[128,768]{1,0:T(8,128)(2,1)}, bf16[128,768]{1,0:T(8,128)(2,1)}, bf16[128,128]{1,0:T(8,128)(2,1)}, bf16[256,128]{1,0:T(8,128)(2,1)}, f32[256,128]{1,0:T(8,128)}) custom-call(s32[2]{0:T(128)} %pad_add_fusion.at_ref.y_ref, s32[2,128]{1,0:T(2,128)} %bitcast.49, f32[1,128]{1,0:T(1,128)} %bitcast.50, bf16[128,384]{1,0:T(8,128)(2,1)} %tokens_ref.1, ...), custom_call_target="tpu_custom_call" | custom-call | flops 1000000 | bytes 20000000 | tf_op jit(solution)/shard_map/pallas_call | solution.py:383
  4.1 1.6 collective-permute-done.got_ref
  6.4 2.6 shard_map.145
  9.1 11.2 %all-to-all-start = ((bf16[16,32,768]{2,0,1:T(8,128)(2,1)}), bf16[16,32,768]{2,0,1:T(8,128)(2,1)}, u32[]{:S(2)}, u32[]{:S(2)}) async-start(bf16[16,32,768]{2,0,1:T(8,128)(2,1)} %bitcast.39), calls=%async_computation | async-start | bytes 1572864 | tf_op jit(solution)/shard_map/all_to_all | solution.py:104
  20.4 2.8 %shard_map.146 = bf16[512,896]{1,0:T(8,128)(2,1)} custom-call(s32[2]{0:T(128)} %pad_add_fusion.at_ref.y_ref, bf16[128,768]{1,0:T(8,128)(2,1)} %get-tuple-element.37.mine_ref, bf16[128,768]{1,0:T(8,128)(2,1)} %copy-done.11, bf16[128,128]{1,0:T(8,128)(2,1)} %get-tuple-element.41.refs_0_), custom_call_target="tpu_custom_call" | custom-call | flops 1000000 | bytes 20000000 | tf_op jit(solution)/shard_map/pallas_call | solution.py:383
  23.3 20.4 %all-to-all-done = bf16[16,32,768]{2,0,1:T(8,128)(2,1)} async-done(((bf16[16,32,768]{2,0,1:T(8,128)(2,1)}), bf16[16,32,768]{2,0,1:T(8,128)(2,1)}, u32[]{:S(2)}, u32[]{:S(2)}) %all-to-all-start) | async-done | bytes 786464 | tf_op jit(solution)/shard_map/all_to_all | solution.py:104
  43.6 5.2 %all-to-all-start.1 = ((bf16[16,32,896]{2,0,1:T(8,128)(2,1)}), bf16[16,32,896]{2,0,1:T(8,128)(2,1)}, u32[]{:S(2)}, u32[]{:S(2)}) async-start(bf16[16,32,896]{2,0,1:T(8,128)(2,1)} %bitcast.38), calls=%async_computation.1 | async-start | bytes 1835008 | tf_op jit(solution)/shard_map/all_to_all | solution.py:104
  50.0 12.8 %all-gather = f32[8,1,384]{2,1,0:T(1,128)S(1)} all-gather(f32[1,1,384]{2,1,0:T(1,128)S(1)} %reshape.100), channel_id=1, replica_groups=mesh['ep_x'=4,'ep_z'=8,'tp_y'=4,'tp_c'=2] {'tp_y','tp_c'}, dimensions={0}, use_global_device_ids=true | all-gather | bytes 13824 | tf_op jit(solution)/shard_map/all_gather | solution.py:470
  64.5 1.3 collective-permute-start.2
  65.8 2.0 collective-permute-start.4
  67.7 6.6 %all-to-all-done.1 = bf16[16,32,896]{2,0,1:T(8,128)(2,1)} async-done(((bf16[16,32,896]{2,0,1:T(8,128)(2,1)}), bf16[16,32,896]{2,0,1:T(8,128)(2,1)}, u32[]{:S(2)}, u32[]{:S(2)}) %all-to-all-start.1) | async-done | bytes 917536 | tf_op jit(solution)/shard_map/all_to_all | solution.py:104
  74.3 1.2 slice.76.refs_0_.refs_5_
  75.5 1.6 collective-permute-start.14
  77.2 9.1 %collective-permute-done.2.refs_2_.refs_4_ = bf16[512,768]{1,0:T(8,128)(2,1)S(1)} collective-permute-done((bf16[512,768]{1,0:T(8,128)(2,1)}, bf16[512,768]{1,0:T(8,128)(2,1)S(1)}, u32[]{:S(2)}, u32[]{:S(2)}) %collective-permute-start.2) | collective-permute-done | bytes 786464 | tf_op jit(solution)/shard_map/ppermute | solution.py:96
  87.3 1.8 collective-permute-start.3
  89.1 1.8 slice.73
  90.9 1.4 collective-permute-start.5
  92.6 8.3 %shard_map.147 = (f32[512,512]{1,0:T(8,128)}, f32[512,512]{1,0:T(8,128)}) custom-call(s32[2]{0:T(128)} %pad_add_fusion.at_ref.y_ref, bf16[512,768]{1,0:T(8,128)(2,1)} %bitcast.7.refs_0_, bf16[512,768]{1,0:T(8,128)(2,1)} %collective-permute-done.4.refs_1_, bf16[512,768]{1,0:T(8,128)(2,1)} %copy-done.13, bf16[256,3072]{1,0:T(8,128)(2,1)} %refs_0_.3, ...), custom_call_target="tpu_custom_call" | custom-call | flops 2415919104 | bytes 20000000 | tf_op jit(solution)/shard_map/pallas_call | solution.py:383
  101.0 2.2 collective-permute-done.14.refs_4_.refs_9_
  104.1 2.7 collective-permute-done.13.refs_1_.refs_6_
  107.6 1.2 collective-permute-start.16
  108.8 2.8 %collective-permute-done.3.refs_0_.refs_2_ = bf16[256,768]{1,0:T(8,128)(2,1)S(1)} collective-permute-done((bf16[256,768]{1,0:T(8,128)(2,1)}, bf16[256,768]{1,0:T(8,128)(2,1)S(1)}, u32[]{:S(2)}, u32[]{:S(2)}) %collective-permute-start.3) | collective-permute-done | bytes 393248 | tf_op jit(solution)/shard_map/ppermute | solution.py:96
  111.6 3.7 %collective-permute-done.5.refs_1_.refs_3_ = bf16[256,768]{1,0:T(8,128)(2,1)} collective-permute-done((bf16[256,768]{1,0:T(8,128)(2,1)}, bf16[256,768]{1,0:T(8,128)(2,1)}, u32[]{:S(2)}, u32[]{:S(2)}) %collective-permute-start.5) | collective-permute-done | bytes 393248 | tf_op jit(solution)/shard_map/ppermute | solution.py:96
  115.3 6.6 %shard_map.148 = (f32[512,512]{1,0:T(8,128)}, f32[512,512]{1,0:T(8,128)}, bf16[512,512]{1,0:T(8,128)(2,1)}, f32[32,128]{1,0:T(8,128)}) custom-call(s32[2]{0:T(128)} %pad_add_fusion.at_ref.y_ref, bf16[256,768]{1,0:T(8,128)(2,1)} %copy-done.12, bf16[256,768]{1,0:T(8,128)(2,1)} %collective-permute-done.5.refs_1_.refs_3_, bf16[256,3072]{1,0:T(8,128)(2,1)} %refs_0_.3, ...), custom_call_target="tpu_custom_call" | custom-call | flops 805306368 | bytes 20000000 | tf_op jit(solution)/shard_map/pallas_call | solution.py:383
  123.6 11.0 %all-to-all-start.3 = ((f32[2,256,32]{2,0,1:T(2,128)}), f32[2,256,32]{2,0,1:T(2,128)S(1)}, u32[]{:S(2)}, u32[]{:S(2)}) async-start(f32[2,256,32]{2,0,1:T(2,128)} %broadcast_in_dim.36), calls=%async_computation.3 | async-start | bytes 524288 | tf_op jit(solution)/shard_map/all_to_all | solution.py:517
  134.6 3.3 %shard_map.150 = (bf16[256,768]{1,0:T(8,128)(2,1)}, bf16[256,768]{1,0:T(8,128)(2,1)}) custom-call(s32[2]{0:T(128)} %pad_add_fusion.at_ref.y_ref, bf16[512,512]{1,0:T(8,128)(2,1)} %get-tuple-element.44.hidden_ref.refs_10_, bf16[256,3072]{1,0:T(8,128)(2,1)} %refs_5_.3, bf16[256,3072]{1,0:T(8,128)(2,1)} %copy-done.1), custom_call_target="tpu_custom_call" | custom-call | flops 402653184 | bytes 20000000 | tf_op jit(solution)/shard_map/pallas_call | solution.py:383
  137.9 2.9 %collective-permute-start.10 = (bf16[256,768]{1,0:T(8,128)(2,1)}, bf16[256,768]{1,0:T(8,128)(2,1)S(1)}, u32[]{:S(2)}, u32[]{:S(2)}) collective-permute-start(bf16[256,768]{1,0:T(8,128)(2,1)} %get-tuple-element.49), channel_id=1, source_target_pairs={{0,6},{2,0},{4,2},{6,4},{1,7},{3,1},{5,3},{7,5},{8,14},{10,8},{12,... | collective-permute-start | bytes 1179656 | tf_op jit(solution)/shard_map/ppermute | solution.py:96
  140.7 6.1 %shard_map.149 = (bf16[512,768]{1,0:T(8,128)(2,1)}, bf16[512,768]{1,0:T(8,128)(2,1)}, bf16[512,768]{1,0:T(8,128)(2,1)}) custom-call(s32[2]{0:T(128)} %pad_add_fusion.at_ref.y_ref, bf16[512,512]{1,0:T(8,128)(2,1)} %get-tuple-element.44.hidden_ref.refs_10_, bf16[256,3072]{1,0:T(8,128)(2,1)} %refs_5_.3, bf16[256,3072]{1,0:T(8,128)(2,1)} %copy-done.1), custom_call_target="tpu_custom_call" | custom-call | flops 1207959552 | bytes 20000000 | tf_op jit(solution)/shard_map/pallas_call | solution.py:383
  146.9 2.1 all-to-all-done.3
  151.1 1.2 add_convert_fusion.7
  152.3 3.3 %collective-permute-start.11 = (bf16[512,768]{1,0:T(8,128)(2,1)S(1)}, bf16[512,768]{1,0:T(8,128)(2,1)S(1)}, u32[]{:S(2)}, u32[]{:S(2)}) collective-permute-start(bf16[512,768]{1,0:T(8,128)(2,1)S(1)} %add_convert_fusion.7), channel_id=1, source_target_pairs={{0,6},{2,0},{4,2},{6,4},{1,7},{3,1},{5,3},{7,5},{8,14},{10,8},{12,... | collective-permute-start | bytes 2359304 | tf_op jit(solution)/shard_map/ppermute | solution.py:96
  155.6 1.0 add_convert_fusion.8
  156.6 7.1 %shard_map.151.refs_7_ = f32[512,512]{1,0:T(8,128)} custom-call(s32[2]{0:T(128)} %pad_add_fusion.at_ref.y_ref, bf16[512,768]{1,0:T(8,128)(2,1)} %copy-done.2, bf16[512,768]{1,0:T(8,128)(2,1)} %copy-done.4, bf16[256,768]{1,0:T(8,128)(2,1)} %collective-permute-done.15.refs_2_.refs_7_, bf16[256,768]{1,0:T(8,128)(2,1)} %collective-permute-done.16.refs_3_.refs_8_, ...), custom_call_target="tpu_custom_call" | custom-call | flops 1610612736 | bytes 20000000 | tf_op jit(solution)/shard_map/pallas_call | solution.py:383
  163.7 5.9 %shard_map.152 = (bf16[512,512]{1,0:T(8,128)(2,1)}, bf16[512,512]{1,0:T(8,128)(2,1)}, f32[512,1]{1,0:T(8,128)}, bf16[256,768]{1,0:T(8,128)(2,1)}, bf16[256,768]{1,0:T(8,128)(2,1)}) custom-call(s32[2]{0:T(128)} %pad_add_fusion.at_ref.y_ref, bf16[256,3072]{1,0:T(8,128)(2,1)} %refs_0_.3, bf16[256,3072]{1,0:T(8,128)(2,1)} %collective-permute-done.6.refs_4_.refs_3_.refs_1_, ...), custom_call_target="tpu_custom_call" | custom-call | flops 805306368 | bytes 20000000 | tf_op jit(solution)/shard_map/pallas_call | solution.py:383
  169.6 3.2 %collective-permute-start.19 = (bf16[256,768]{1,0:T(8,128)(2,1)}, bf16[256,768]{1,0:T(8,128)(2,1)}, u32[]{:S(2)}, u32[]{:S(2)}) collective-permute-start(bf16[256,768]{1,0:T(8,128)(2,1)} %get-tuple-element.61), channel_id=1, source_target_pairs={{0,6},{2,0},{4,2},{6,4},{1,7},{3,1},{5,3},{7,5},{8,14},{10,8},{12,... | collective-permute-start | bytes 1179656 | tf_op jit(solution)/shard_map/ppermute | solution.py:96
  172.8 14.9 %shard_map.154 = (bf16[768,3072]{1,0:T(8,128)(2,1)}, bf16[768,3072]{1,0:T(8,128)(2,1)}) custom-call(s32[2]{0:T(128)} %pad_add_fusion.at_ref.y_ref, bf16[512,768]{1,0:T(8,128)(2,1)} %bitcast.7.refs_0_, bf16[512,768]{1,0:T(8,128)(2,1)} %collective-permute-done.4.refs_1_, bf16[256,768]{1,0:T(8,128)(2,1)} %copy-done.12, ...), custom_call_target="tpu_custom_call" | custom-call | flops 4831838208 | bytes 20000000 | tf_op jit(solution)/shard_map/pallas_call | solution.py:383
  188.0 7.8 %shard_map.153 = (bf16[512,768]{1,0:T(8,128)(2,1)}, bf16[512,768]{1,0:T(8,128)(2,1)}, bf16[512,768]{1,0:T(8,128)(2,1)}) custom-call(s32[2]{0:T(128)} %pad_add_fusion.at_ref.y_ref, bf16[256,3072]{1,0:T(8,128)(2,1)} %refs_0_.3, bf16[256,3072]{1,0:T(8,128)(2,1)} %collective-permute-done.6.refs_4_.refs_3_.refs_1_, bf16[256,3072]{1,0:T(8,128)(2,1)} %refs_2_.5, ...), custom_call_target="tpu_custom_call" | custom-call | flops 2415919104 | bytes 20000000 | tf_op jit(solution)/shard_map/pallas_call | solution.py:383
  195.8 1.2 add_convert_fusion.6
  197.0 9.8 %all-to-all-start.2 = ((bf16[16,32,768]{2,0,1:T(8,128)(2,1)}), bf16[16,32,768]{2,0,1:T(8,128)(2,1)S(1)}, u32[]{:S(2)}, u32[]{:S(2)}) async-start(bf16[16,32,768]{2,0,1:T(8,128)(2,1)} %bitcast.15), calls=%async_computation.2 | async-start | bytes 1572864 | tf_op jit(solution)/shard_map/all_to_all | solution.py:104
  206.8 1.2 add_convert_fusion.4
  207.9 3.1 %collective-permute-start.20 = (bf16[512,768]{1,0:T(8,128)(2,1)S(1)}, bf16[512,768]{1,0:T(8,128)(2,1)S(1)}, u32[]{:S(2)}, u32[]{:S(2)}) collective-permute-start(bf16[512,768]{1,0:T(8,128)(2,1)S(1)} %add_convert_fusion.4), channel_id=1, source_target_pairs={{0,6},{2,0},{4,2},{6,4},{1,7},{3,1},{5,3},{7,5},{8,14},{10,8},{12,... | collective-permute-start | bytes 2359304 | tf_op jit(solution)/shard_map/ppermute | solution.py:96
  211.0 1.1 add_convert_fusion.5
  212.2 15.7 %collective-permute-done.20 = bf16[512,768]{1,0:T(8,128)(2,1)S(1)} collective-permute-done((bf16[512,768]{1,0:T(8,128)(2,1)S(1)}, bf16[512,768]{1,0:T(8,128)(2,1)S(1)}, u32[]{:S(2)}, u32[]{:S(2)}) %collective-permute-start.20) | collective-permute-done | bytes 786464 | tf_op jit(solution)/shard_map/ppermute | solution.py:96
  227.9 4.6 %collective-permute-done.18 = bf16[512,768]{1,0:T(8,128)(2,1)S(1)} collective-permute-done((bf16[512,768]{1,0:T(8,128)(2,1)S(1)}, bf16[512,768]{1,0:T(8,128)(2,1)S(1)}, u32[]{:S(2)}, u32[]{:S(2)}) %collective-permute-start.18) | collective-permute-done | bytes 786464 | tf_op jit(solution)/shard_map/ppermute | solution.py:96
  232.5 1.2 add_convert_fusion.3
  233.7 9.8 %all-to-all-start.4 = ((bf16[16,32,768]{2,0,1:T(8,128)(2,1)}), bf16[16,32,768]{2,0,1:T(8,128)(2,1)S(1)}, u32[]{:S(2)}, u32[]{:S(2)}) async-start(bf16[16,32,768]{2,0,1:T(8,128)(2,1)} %bitcast.21), calls=%async_computation.4 | async-start | bytes 1572864 | tf_op jit(solution)/shard_map/all_to_all | solution.py:104
  245.1 20.5 %all-to-all-done.4 = bf16[16,32,768]{2,0,1:T(8,128)(2,1)S(1)} async-done(((bf16[16,32,768]{2,0,1:T(8,128)(2,1)}), bf16[16,32,768]{2,0,1:T(8,128)(2,1)S(1)}, u32[]{:S(2)}, u32[]{:S(2)}) %all-to-all-start.4) | async-done | bytes 786464 | tf_op jit(solution)/shard_map/all_to_all | solution.py:104
  268.0 5.9 %add_convert_fusion = (bf16[256,3072]{1,0:T(8,128)(2,1)}, bf16[256,3072]{1,0:T(8,128)(2,1)}, bf16[256,3072]{1,0:T(8,128)(2,1)}) fusion(bf16[768,3072]{1,0:T(8,128)(2,1)} %collective-permute-done.22, bf16[768,3072]{1,0:T(8,128)(2,1)} %get-tuple-element.63), kind=kLoop, calls=%fused_computation | loop fusion | flops 9437184 | bytes 14155776 | tf_op jit(solution)/shard_map/convert_element_type | solution.py:118
  (108 shorter events, 14.7 us)
Async XLA Ops:
  0.6 19.7 %copy-start = (bf16[256,3072]{1,0:T(8,128)(2,1)S(1)}, bf16[256,3072]{1,0:T(8,128)(2,1)}, u32[]{:S(2)}) copy-start(bf16[256,3072]{1,0:T(8,128)(2,1)} %refs_5_.3) | copy-start | bytes 4718596
  4.1 1.7 collective-permute-start
  9.1 34.6 %all-to-all-start = ((bf16[16,32,768]{2,0,1:T(8,128)(2,1)}), bf16[16,32,768]{2,0,1:T(8,128)(2,1)}, u32[]{:S(2)}, u32[]{:S(2)}) async-start(bf16[16,32,768]{2,0,1:T(8,128)(2,1)} %bitcast.39), calls=%async_computation | async-start | bytes 1572864 | tf_op jit(solution)/shard_map/all_to_all | solution.py:104
  20.3 42.4 %collective-permute-start.1 = (bf16[256,3072]{1,0:T(8,128)(2,1)S(1)}, bf16[256,3072]{1,0:T(8,128)(2,1)S(1)}, u32[]{:S(2)}, u32[]{:S(2)}) collective-permute-start(bf16[256,3072]{1,0:T(8,128)(2,1)S(1)} %copy-done), channel_id=1, source_target_pairs={{0,1},{1,0},{2,3},{3,2},{4,5},{5,4},{6,7},{7,6},{8,9},{9,8},{10,11... | collective-permute-start | bytes 4718600 | tf_op jit(solution)/shard_map/ppermute | solution.py:100
  20.4 29.0 %copy-start.17 = (f32[384]{0:T(512)S(1)}, f32[384]{0:T(512)}, u32[]{:S(2)}) copy-start(f32[384]{0:T(512)} %param.15) | copy-start | bytes 4612
  20.4 29.0 %copy-start.5 = (bf16[128,384]{1,0:T(8,128)(2,1)S(1)}, bf16[128,384]{1,0:T(8,128)(2,1)}, u32[]{:S(2)}) copy-start(bf16[128,384]{1,0:T(8,128)(2,1)} %tokens_ref.1) | copy-start | bytes 294916
  43.6 30.7 %all-to-all-start.1 = ((bf16[16,32,896]{2,0,1:T(8,128)(2,1)}), bf16[16,32,896]{2,0,1:T(8,128)(2,1)}, u32[]{:S(2)}, u32[]{:S(2)}) async-start(bf16[16,32,896]{2,0,1:T(8,128)(2,1)} %bitcast.38), calls=%async_computation.1 | async-start | bytes 1835008 | tf_op jit(solution)/shard_map/all_to_all | solution.py:104
  48.8 42.1 %collective-permute-start.6 = (bf16[256,3072]{1,0:T(8,128)(2,1)}, bf16[256,3072]{1,0:T(8,128)(2,1)}, u32[]{:S(2)}, u32[]{:S(2)}) collective-permute-start(bf16[256,3072]{1,0:T(8,128)(2,1)} %refs_0_.3), channel_id=1, source_target_pairs={{0,1},{1,0},{2,3},{3,2},{4,5},{5,4},{6,7},{7,6},{8,9},{9,8},{10,11... | collective-permute-start | bytes 4718600 | tf_op jit(solution)/shard_map/ppermute | solution.py:100
  48.9 43.7 %collective-permute-start.7 = (bf16[256,3072]{1,0:T(8,128)(2,1)}, bf16[256,3072]{1,0:T(8,128)(2,1)}, u32[]{:S(2)}, u32[]{:S(2)}) collective-permute-start(bf16[256,3072]{1,0:T(8,128)(2,1)} %refs_2_.5), channel_id=1, source_target_pairs={{0,1},{1,0},{2,3},{3,2},{4,5},{5,4},{6,7},{7,6},{8,9},{9,8},{10,11... | collective-permute-start | bytes 4718600 | tf_op jit(solution)/shard_map/ppermute | solution.py:100
  62.8 0.7 copy-start.16
  62.8 1.1 copy-start.1
  64.5 21.8 %collective-permute-start.2 = (bf16[512,768]{1,0:T(8,128)(2,1)}, bf16[512,768]{1,0:T(8,128)(2,1)S(1)}, u32[]{:S(2)}, u32[]{:S(2)}) collective-permute-start(bf16[512,768]{1,0:T(8,128)(2,1)} %bitcast.7.refs_0_), channel_id=1, source_target_pairs={{0,2},{2,4},{4,6},{6,0},{1,3},{3,5},{5,7},{7,1},{8,10},{10,12},{12... | collective-permute-start | bytes 2359304 | tf_op jit(solution)/shard_map/ppermute | solution.py:96
  65.8 21.6 %collective-permute-start.4 = (bf16[512,768]{1,0:T(8,128)(2,1)}, bf16[512,768]{1,0:T(8,128)(2,1)}, u32[]{:S(2)}, u32[]{:S(2)}) collective-permute-start(bf16[512,768]{1,0:T(8,128)(2,1)} %bitcast.7.refs_0_), channel_id=1, source_target_pairs={{0,6},{2,0},{4,2},{6,4},{1,7},{3,1},{5,3},{7,5},{8,14},{10,8},{12,... | collective-permute-start | bytes 2359304 | tf_op jit(solution)/shard_map/ppermute | solution.py:96
  74.3 18.0 %copy-start.20 = (s32[64]{0:T(128)S(1)}, s32[64]{0:T(128)}, u32[]{:S(2)}) copy-start(s32[64]{0:T(128)} %param.17) | copy-start | bytes 772
  75.5 25.4 %copy-start.2 = (bf16[512,768]{1,0:T(8,128)(2,1)}, bf16[512,768]{1,0:T(8,128)(2,1)S(1)}, u32[]{:S(2)}) copy-start(bf16[512,768]{1,0:T(8,128)(2,1)S(1)} %slice.76.refs_0_.refs_5_) | copy-start | bytes 2359300
  75.5 27.6 %collective-permute-start.14 = (bf16[512,768]{1,0:T(8,128)(2,1)S(1)}, bf16[512,768]{1,0:T(8,128)(2,1)S(1)}, u32[]{:S(2)}, u32[]{:S(2)}) collective-permute-start(bf16[512,768]{1,0:T(8,128)(2,1)S(1)} %slice.76.refs_0_.refs_5_), channel_id=1, source_target_pairs={{0,2},{2,4},{4,6},{6,0},{1,3},{3,5},{5,7},{7,1},{8,10},{10,12},{12... | collective-permute-start | bytes 2359304 | tf_op jit(solution)/shard_map/ppermute | solution.py:96
  86.3 1.0 copy-start.13
  86.3 20.4 %collective-permute-start.13 = (bf16[512,768]{1,0:T(8,128)(2,1)S(1)}, bf16[512,768]{1,0:T(8,128)(2,1)S(1)}, u32[]{:S(2)}, u32[]{:S(2)}) collective-permute-start(bf16[512,768]{1,0:T(8,128)(2,1)S(1)} %slice.76.refs_0_.refs_5_), channel_id=1, source_target_pairs={{0,6},{2,0},{4,2},{6,4},{1,7},{3,1},{5,3},{7,5},{8,14},{10,8},{12,... | collective-permute-start | bytes 2359304 | tf_op jit(solution)/shard_map/ppermute | solution.py:96
  87.3 24.3 %collective-permute-start.3 = (bf16[256,768]{1,0:T(8,128)(2,1)}, bf16[256,768]{1,0:T(8,128)(2,1)S(1)}, u32[]{:S(2)}, u32[]{:S(2)}) collective-permute-start(bf16[256,768]{1,0:T(8,128)(2,1)} %slice.72), channel_id=1, source_target_pairs={{0,2},{2,4},{4,6},{6,0},{1,3},{3,5},{5,7},{7,1},{8,10},{10,12},{12... | collective-permute-start | bytes 1179656 | tf_op jit(solution)/shard_map/ppermute | solution.py:96
  90.9 24.4 %collective-permute-start.5 = (bf16[256,768]{1,0:T(8,128)(2,1)}, bf16[256,768]{1,0:T(8,128)(2,1)}, u32[]{:S(2)}, u32[]{:S(2)}) collective-permute-start(bf16[256,768]{1,0:T(8,128)(2,1)} %slice.73), channel_id=1, source_target_pairs={{0,6},{2,0},{4,2},{6,4},{1,7},{3,1},{5,3},{7,5},{8,14},{10,8},{12,... | collective-permute-start | bytes 1179656 | tf_op jit(solution)/shard_map/ppermute | solution.py:96
  103.2 18.7 %copy-start.3 = (bf16[512,768]{1,0:T(8,128)(2,1)}, bf16[512,768]{1,0:T(8,128)(2,1)S(1)}, u32[]{:S(2)}) copy-start(bf16[512,768]{1,0:T(8,128)(2,1)S(1)} %collective-permute-done.14.refs_4_.refs_9_) | copy-start | bytes 2359300
  104.0 52.6 %collective-permute-start.15 = (bf16[256,768]{1,0:T(8,128)(2,1)}, bf16[256,768]{1,0:T(8,128)(2,1)}, u32[]{:S(2)}, u32[]{:S(2)}) collective-permute-start(bf16[256,768]{1,0:T(8,128)(2,1)} %slice.77), channel_id=1, source_target_pairs={{0,2},{2,4},{4,6},{6,0},{1,3},{3,5},{5,7},{7,1},{8,10},{10,12},{12... | collective-permute-start | bytes 1179656 | tf_op jit(solution)/shard_map/ppermute | solution.py:96
  106.7 15.1 %copy-start.4 = (bf16[512,768]{1,0:T(8,128)(2,1)}, bf16[512,768]{1,0:T(8,128)(2,1)S(1)}, u32[]{:S(2)}) copy-start(bf16[512,768]{1,0:T(8,128)(2,1)S(1)} %collective-permute-done.13.refs_1_.refs_6_) | copy-start | bytes 2359300
  107.6 49.1 %collective-permute-start.16 = (bf16[256,768]{1,0:T(8,128)(2,1)}, bf16[256,768]{1,0:T(8,128)(2,1)}, u32[]{:S(2)}, u32[]{:S(2)}) collective-permute-start(bf16[256,768]{1,0:T(8,128)(2,1)} %slice.78), channel_id=1, source_target_pairs={{0,6},{2,0},{4,2},{6,4},{1,7},{3,1},{5,3},{7,5},{8,14},{10,8},{12,... | collective-permute-start | bytes 1179656 | tf_op jit(solution)/shard_map/ppermute | solution.py:96
  111.6 3.7 %copy-start.12 = (bf16[256,768]{1,0:T(8,128)(2,1)}, bf16[256,768]{1,0:T(8,128)(2,1)S(1)}, u32[]{:S(2)}) copy-start(bf16[256,768]{1,0:T(8,128)(2,1)S(1)} %collective-permute-done.3.refs_0_.refs_2_) | copy-start | bytes 1179652
  123.6 25.5 %all-to-all-start.3 = ((f32[2,256,32]{2,0,1:T(2,128)}), f32[2,256,32]{2,0,1:T(2,128)S(1)}, u32[]{:S(2)}, u32[]{:S(2)}) async-start(f32[2,256,32]{2,0,1:T(2,128)} %broadcast_in_dim.36), calls=%async_computation.3 | async-start | bytes 524288 | tf_op jit(solution)/shard_map/all_to_all | solution.py:517
  137.9 13.2 %collective-permute-start.10 = (bf16[256,768]{1,0:T(8,128)(2,1)}, bf16[256,768]{1,0:T(8,128)(2,1)S(1)}, u32[]{:S(2)}, u32[]{:S(2)}) collective-permute-start(bf16[256,768]{1,0:T(8,128)(2,1)} %get-tuple-element.49), channel_id=1, source_target_pairs={{0,6},{2,0},{4,2},{6,4},{1,7},{3,1},{5,3},{7,5},{8,14},{10,8},{12,... | collective-permute-start | bytes 1179656 | tf_op jit(solution)/shard_map/ppermute | solution.py:96
  140.7 14.9 %collective-permute-start.8 = (bf16[256,768]{1,0:T(8,128)(2,1)}, bf16[256,768]{1,0:T(8,128)(2,1)S(1)}, u32[]{:S(2)}, u32[]{:S(2)}) collective-permute-start(bf16[256,768]{1,0:T(8,128)(2,1)} %get-tuple-element.47), channel_id=1, source_target_pairs={{0,2},{2,4},{4,6},{6,0},{1,3},{3,5},{5,7},{7,1},{8,10},{10,12},{12... | collective-permute-start | bytes 1179656 | tf_op jit(solution)/shard_map/ppermute | solution.py:96
  146.9 8.7 %copy-start.8 = (bf16[512,768]{1,0:T(8,128)(2,1)S(1)}, bf16[512,768]{1,0:T(8,128)(2,1)}, u32[]{:S(2)}) copy-start(bf16[512,768]{1,0:T(8,128)(2,1)} %get-tuple-element.46) | copy-start | bytes 2359300
  149.4 7.2 %copy-start.18 = (f32[64]{0:T(128)}, f32[64]{0:T(128)S(1)}, u32[]{:S(2)}) copy-start(f32[64]{0:T(128)S(1)} %div.26) | copy-start | bytes 772
  152.3 43.5 %collective-permute-start.11 = (bf16[512,768]{1,0:T(8,128)(2,1)S(1)}, bf16[512,768]{1,0:T(8,128)(2,1)S(1)}, u32[]{:S(2)}, u32[]{:S(2)}) collective-permute-start(bf16[512,768]{1,0:T(8,128)(2,1)S(1)} %add_convert_fusion.7), channel_id=1, source_target_pairs={{0,6},{2,0},{4,2},{6,4},{1,7},{3,1},{5,3},{7,5},{8,14},{10,8},{12,... | collective-permute-start | bytes 2359304 | tf_op jit(solution)/shard_map/ppermute | solution.py:96
  156.6 39.2 %collective-permute-start.9 = (bf16[512,768]{1,0:T(8,128)(2,1)}, bf16[512,768]{1,0:T(8,128)(2,1)S(1)}, u32[]{:S(2)}, u32[]{:S(2)}) collective-permute-start(bf16[512,768]{1,0:T(8,128)(2,1)} %add_convert_fusion.8), channel_id=1, source_target_pairs={{0,2},{2,4},{4,6},{6,0},{1,3},{3,5},{5,7},{7,1},{8,10},{10,12},{12... | collective-permute-start | bytes 2359304 | tf_op jit(solution)/shard_map/ppermute | solution.py:96
  169.6 37.1 %collective-permute-start.19 = (bf16[256,768]{1,0:T(8,128)(2,1)}, bf16[256,768]{1,0:T(8,128)(2,1)}, u32[]{:S(2)}, u32[]{:S(2)}) collective-permute-start(bf16[256,768]{1,0:T(8,128)(2,1)} %get-tuple-element.61), channel_id=1, source_target_pairs={{0,6},{2,0},{4,2},{6,4},{1,7},{3,1},{5,3},{7,5},{8,14},{10,8},{12,... | collective-permute-start | bytes 1179656 | tf_op jit(solution)/shard_map/ppermute | solution.py:96
  172.8 38.2 %collective-permute-start.17 = (bf16[256,768]{1,0:T(8,128)(2,1)}, bf16[256,768]{1,0:T(8,128)(2,1)}, u32[]{:S(2)}, u32[]{:S(2)}) collective-permute-start(bf16[256,768]{1,0:T(8,128)(2,1)} %get-tuple-element.59), channel_id=1, source_target_pairs={{0,2},{2,4},{4,6},{6,0},{1,3},{3,5},{5,7},{7,1},{8,10},{10,12},{12... | collective-permute-start | bytes 1179656 | tf_op jit(solution)/shard_map/ppermute | solution.py:96
  187.7 8.1 %copy-start.6 = (bf16[512,768]{1,0:T(8,128)(2,1)S(1)}, bf16[512,768]{1,0:T(8,128)(2,1)}, u32[]{:S(2)}) copy-start(bf16[512,768]{1,0:T(8,128)(2,1)} %get-tuple-element.45) | copy-start | bytes 2359300
  187.7 80.3 %collective-permute-start.22 = (bf16[768,3072]{1,0:T(8,128)(2,1)}, bf16[768,3072]{1,0:T(8,128)(2,1)}, u32[]{:S(2)}, u32[]{:S(2)}) collective-permute-start(bf16[768,3072]{1,0:T(8,128)(2,1)} %get-tuple-element.64), channel_id=1, source_target_pairs={{0,1},{1,0},{2,3},{3,2},{4,5},{5,4},{6,7},{7,6},{8,9},{9,8},{10,11... | collective-permute-start | bytes 14155784 | tf_op jit(solution)/shard_map/ppermute | solution.py:100
  197.0 9.8 %copy-start.10 = (bf16[512,768]{1,0:T(8,128)(2,1)S(1)}, bf16[512,768]{1,0:T(8,128)(2,1)}, u32[]{:S(2)}) copy-start(bf16[512,768]{1,0:T(8,128)(2,1)} %get-tuple-element.60) | copy-start | bytes 2359300
  197.0 14.0 %copy-start.9 = (bf16[512,768]{1,0:T(8,128)(2,1)S(1)}, bf16[512,768]{1,0:T(8,128)(2,1)}, u32[]{:S(2)}) copy-start(bf16[512,768]{1,0:T(8,128)(2,1)} %get-tuple-element.58) | copy-start | bytes 2359300
  197.0 36.7 %all-to-all-start.2 = ((bf16[16,32,768]{2,0,1:T(8,128)(2,1)}), bf16[16,32,768]{2,0,1:T(8,128)(2,1)S(1)}, u32[]{:S(2)}, u32[]{:S(2)}) async-start(bf16[16,32,768]{2,0,1:T(8,128)(2,1)} %bitcast.15), calls=%async_computation.2 | async-start | bytes 1572864 | tf_op jit(solution)/shard_map/all_to_all | solution.py:104
  206.8 25.7 %copy-start.7 = (bf16[512,768]{1,0:T(8,128)(2,1)S(1)}, bf16[512,768]{1,0:T(8,128)(2,1)}, u32[]{:S(2)}) copy-start(bf16[512,768]{1,0:T(8,128)(2,1)} %get-tuple-element.57) | copy-start | bytes 2359300
  207.9 20.0 %collective-permute-start.20 = (bf16[512,768]{1,0:T(8,128)(2,1)S(1)}, bf16[512,768]{1,0:T(8,128)(2,1)S(1)}, u32[]{:S(2)}, u32[]{:S(2)}) collective-permute-start(bf16[512,768]{1,0:T(8,128)(2,1)S(1)} %add_convert_fusion.4), channel_id=1, source_target_pairs={{0,6},{2,0},{4,2},{6,4},{1,7},{3,1},{5,3},{7,5},{8,14},{10,8},{12,... | collective-permute-start | bytes 2359304 | tf_op jit(solution)/shard_map/ppermute | solution.py:96
  212.1 20.4 %collective-permute-start.18 = (bf16[512,768]{1,0:T(8,128)(2,1)S(1)}, bf16[512,768]{1,0:T(8,128)(2,1)S(1)}, u32[]{:S(2)}, u32[]{:S(2)}) collective-permute-start(bf16[512,768]{1,0:T(8,128)(2,1)S(1)} %add_convert_fusion.5), channel_id=1, source_target_pairs={{0,2},{2,4},{4,6},{6,0},{1,3},{3,5},{5,7},{7,1},{8,10},{10,12},{12... | collective-permute-start | bytes 2359304 | tf_op jit(solution)/shard_map/ppermute | solution.py:96
  233.7 31.9 %all-to-all-start.4 = ((bf16[16,32,768]{2,0,1:T(8,128)(2,1)}), bf16[16,32,768]{2,0,1:T(8,128)(2,1)S(1)}, u32[]{:S(2)}, u32[]{:S(2)}) async-start(bf16[16,32,768]{2,0,1:T(8,128)(2,1)} %bitcast.21), calls=%async_computation.4 | async-start | bytes 1572864 | tf_op jit(solution)/shard_map/all_to_all | solution.py:104
  243.5 22.4 %copy-start.14 = (f32[256,128]{1,0:T(8,128)S(1)}, f32[256,128]{1,0:T(8,128)}, u32[]{:S(2)}) copy-start(f32[256,128]{1,0:T(8,128)} %get-tuple-element.36) | copy-start | bytes 393220
  243.6 23.5 %copy-start.15 = (bf16[128,384]{1,0:T(8,128)(2,1)S(1)}, bf16[128,384]{1,0:T(8,128)(2,1)}, u32[]{:S(2)}) copy-start(bf16[128,384]{1,0:T(8,128)(2,1)} %upstream_ref.1) | copy-start | bytes 294916
  243.6 23.5 %copy-start.19 = (bf16[256,128]{1,0:T(8,128)(2,1)S(1)}, bf16[256,128]{1,0:T(8,128)(2,1)}, u32[]{:S(2)}) copy-start(bf16[256,128]{1,0:T(8,128)(2,1)} %get-tuple-element.52) | copy-start | bytes 196612
  243.6 1.4 collective-permute-start.12
  265.7 1.4 collective-permute-start.21
  (1 other events, 0.7 us)
where the time goes:
time: 277 us; the launch traced here: 275 us
  waiting for transfers between devices  93 us (34%)
  starting transfers between devices  70.1 us (25%)
  Pallas kernels  68.2 us (25%)
  other arithmetic  16.5 us (6%)
  blocking collectives  12.8 us (5%)
  local copies, waits for them, and re-layouts  9.99 us (4%)
  between operations  2.77 us (1%)
    pallas_call x11, Pallas kernels, call(): pl.pallas_call(kernel, grid_spec=pltpu.PrefetchScalarGridSpec(num_scalar_...  68.2 us
    all_to_all x4, waiting for transfers between devices, exchange(): lax.all_to_all(blocks.transpose(1, 0, 2), EP, split_axis=1, concat_axis=1...  47.5 us
    ppermute x16, waiting for transfers between devices, rot(): return lax.ppermute(value, 'tp_y', [(i, (i + shift) % 4) for i in range(4)])  40.9 us
    all_to_all x4, starting transfers between devices, exchange(): lax.all_to_all(blocks.transpose(1, 0, 2), EP, split_axis=1, concat_axis=1...  36 us
    ppermute x16, starting transfers between devices, rot(): return lax.ppermute(value, 'tp_y', [(i, (i + shift) % 4) for i in range(4)])  21.9 us
    all_gather x1, blocking collectives, layer(): head = lax.all_gather(reward_head, TP, axis=0, tiled=True)  12.8 us
    convert_element_type x7, other arithmetic, add(): sum((t.astype(f32) for t in terms[1:]), terms[0].astype(f32)).astype(bf16)  12.7 us
    all_to_all x1, starting transfers between devices, layer(): lax.all_to_all(spread, EP_TP, split_axis=1, concat_axis=1, tiled=True)  11 us
  transfers between devices with their start and end apart: 28, of which 14 were waited for; matrix products, arithmetic and copies ran while one was open for 7% of the time, Pallas kernels for 23%

commit v1 on v0

--- a/solution.py
+++ b/solution.py
@@ -234,25 +234,18 @@
 def down_kernel(y_ref, hidden_ref, wd0, wd1, low_ref, high_ref):
     width, half = wd0.shape[0], low_ref.shape[0]
     left, right = pl.ds(0, width), pl.ds(width, width)
-    for i, ref in enumerate((low_ref, high_ref)):
-        at = pl.ds(i * half, half)
-        ref[...] = (
-            plain(hidden_ref[at, left], wd0[...]) + plain(hidden_ref[at, right], wd1[...])
-        ).astype(bf16)
+    total = plain(hidden_ref[:, left], wd0[...]) + plain(hidden_ref[:, right], wd1[...])
+    low_ref[...] = total[:half].astype(bf16)
+    high_ref[...] = total[half:].astype(bf16)
 
 
 def side_kernel(y_ref, hidden_ref, wd0, wd1, *refs):
     out_refs, rows = refs[:3], refs[3]
     width = wd0.shape[0]
     left, right = pl.ds(0, width), pl.ds(width, width)
-    chunk = rows.shape[0] // 2
-
-    @pl.loop(0, 2)
-    def _(i):
-        at = pl.ds(pl.multiple_of(i * chunk, chunk), chunk)
-        rows[at] = (
-            plain(hidden_ref[at, left], wd0[...]) + plain(hidden_ref[at, right], wd1[...])
-        ).astype(bf16)
+    rows[...] = (
+        plain(hidden_ref[:, left], wd0[...]) + plain(hidden_ref[:, right], wd1[...])
+    ).astype(bf16)
 
     for k, ref in enumerate(out_refs):
 
@@ -299,14 +292,14 @@
         gate_grad_ref[at] = (hidden_grad * slope_ref[at]).astype(bf16)
         up_grad_ref[at] = (hidden_grad * silu_ref[at]).astype(bf16)
 
-    for i, ref in enumerate((low_ref, high_ref)):
-        at = pl.ds(i * half, half)
-        ref[...] = (
-            plain(gate_grad_ref[at, left], wg0[...])
-            + plain(gate_grad_ref[at, right], wg1[...])
-            + plain(up_grad_ref[at, left], wu0[...])
-            + plain(up_grad_ref[at, right], wu1[...])
-        ).astype(bf16)
+    total = (
+        plain(gate_grad_ref[:, left], wg0[...])
+        + plain(gate_grad_ref[:, right], wg1[...])
+        + plain(up_grad_ref[:, left], wu0[...])
+        + plain(up_grad_ref[:, right], wu1[...])
+    )
+    low_ref[...] = total[:half].astype(bf16)
+    high_ref[...] = total[half:].astype(bf16)
 
 
 def rest_kernel(y_ref, *refs):
@@ -314,17 +307,12 @@
     out_refs, rows = refs[6:9], refs[9]
     width = wg0.shape[0]
     left, right = pl.ds(0, width), pl.ds(width, width)
-    chunk = rows.shape[0] // 2
-
-    @pl.loop(0, 2)
-    def _(i):
-        at = pl.ds(pl.multiple_of(i * chunk, chunk), chunk)
-        rows[at] = (
-            plain(gate_grad_ref[at, left], wg0[...])
-            + plain(gate_grad_ref[at, right], wg1[...])
-            + plain(up_grad_ref[at, left], wu0[...])
-            + plain(up_grad_ref[at, right], wu1[...])
-        ).astype(bf16)
+    rows[...] = (
+        plain(gate_grad_ref[:, left], wg0[...])
+        + plain(gate_grad_ref[:, right], wg1[...])
+        + plain(up_grad_ref[:, left], wu0[...])
+        + plain(up_grad_ref[:, right], wu1[...])
+    ).astype(bf16)
 
     for k, ref in enumerate(out_refs):
 

time: 277 us -> 277 us (level)
  no operation moved by 1% of the time
where the time goes in v1:
time: 277 us; the launch traced here: 274 us
  waiting for transfers between devices  93 us (34%)
  starting transfers between devices  69.9 us (25%)
  Pallas kernels  67.7 us (24%)
  other arithmetic  16.5 us (6%)
  blocking collectives  12.8 us (5%)
  local copies, waits for them, and re-layouts  9.99 us (4%)
  between operations  2.77 us (1%)
    pallas_call x11, Pallas kernels, call(): pl.pallas_call(kernel, grid_spec=pltpu.PrefetchScalarGridSpec(num_scalar_...  67.7 us
    all_to_all x4, waiting for transfers between devices, exchange(): lax.all_to_all(blocks.transpose(1, 0, 2), EP, split_axis=1, concat_axis=1...  47.4 us
    ppermute x16, waiting for transfers between devices, rot(): return lax.ppermute(value, 'tp_y', [(i, (i + shift) % 4) for i in range(4)])  40.7 us
    all_to_all x4, starting transfers between devices, exchange(): lax.all_to_all(blocks.transpose(1, 0, 2), EP, split_axis=1, concat_axis=1...  36 us
    ppermute x16, starting transfers between devices, rot(): return lax.ppermute(value, 'tp_y', [(i, (i + shift) % 4) for i in range(4)])  22 us
    all_gather x1, blocking collectives, layer(): head = lax.all_gather(reward_head, TP, axis=0, tiled=True)  12.8 us
    convert_element_type x7, other arithmetic, add(): sum((t.astype(f32) for t in terms[1:]), terms[0].astype(f32)).astype(bf16)  12.7 us
    all_to_all x1, starting transfers between devices, layer(): lax.all_to_all(spread, EP_TP, split_axis=1, concat_axis=1, tiled=True)  11 us
  transfers between devices with their start and end apart: 28, of which 14 were waited for; matrix products, arithmetic and copies ran while one was open for 7% of the time, Pallas kernels for 23%

profile of v1, /device:TPU:32, one launch (start us, length us, event | category | flops | bytes accessed | tf_op | source)
XLA Modules:
  0.0 274.3 jit_solution(6673151927481262140)
XLA Ops:
  1.3 2.8 %shard_map.144 = (bf16[128,768]{1,0:T(8,128)(2,1)}, bf16[128,768]{1,0:T(8,128)(2,1)}, bf16[128,128]{1,0:T(8,128)(2,1)}, bf16[256,128]{1,0:T(8,128)(2,1)}, f32[256,128]{1,0:T(8,128)}) custom-call(s32[2]{0:T(128)} %pad_add_fusion.at_ref.y_ref, s32[2,128]{1,0:T(2,128)} %bitcast.49, f32[1,128]{1,0:T(1,128)} %bitcast.50, bf16[128,384]{1,0:T(8,128)(2,1)} %tokens_ref.1, ...), custom_call_target="tpu_custom_call" | custom-call | flops 1000000 | bytes 20000000 | tf_op jit(solution)/shard_map/pallas_call | solution.py:371
  4.1 1.6 collective-permute-done.got_ref
  6.4 2.6 shard_map.145
  9.1 11.2 %all-to-all-start = ((bf16[16,32,768]{2,0,1:T(8,128)(2,1)}), bf16[16,32,768]{2,0,1:T(8,128)(2,1)}, u32[]{:S(2)}, u32[]{:S(2)}) async-start(bf16[16,32,768]{2,0,1:T(8,128)(2,1)} %bitcast.39), calls=%async_computation | async-start | bytes 1572864 | tf_op jit(solution)/shard_map/all_to_all | solution.py:104
  20.4 2.8 %shard_map.146 = bf16[512,896]{1,0:T(8,128)(2,1)} custom-call(s32[2]{0:T(128)} %pad_add_fusion.at_ref.y_ref, bf16[128,768]{1,0:T(8,128)(2,1)} %get-tuple-element.37.mine_ref, bf16[128,768]{1,0:T(8,128)(2,1)} %copy-done.11, bf16[128,128]{1,0:T(8,128)(2,1)} %get-tuple-element.41.refs_0_), custom_call_target="tpu_custom_call" | custom-call | flops 1000000 | bytes 20000000 | tf_op jit(solution)/shard_map/pallas_call | solution.py:371
  23.3 20.4 %all-to-all-done = bf16[16,32,768]{2,0,1:T(8,128)(2,1)} async-done(((bf16[16,32,768]{2,0,1:T(8,128)(2,1)}), bf16[16,32,768]{2,0,1:T(8,128)(2,1)}, u32[]{:S(2)}, u32[]{:S(2)}) %all-to-all-start) | async-done | bytes 786464 | tf_op jit(solution)/shard_map/all_to_all | solution.py:104
  43.6 5.2 %all-to-all-start.1 = ((bf16[16,32,896]{2,0,1:T(8,128)(2,1)}), bf16[16,32,896]{2,0,1:T(8,128)(2,1)}, u32[]{:S(2)}, u32[]{:S(2)}) async-start(bf16[16,32,896]{2,0,1:T(8,128)(2,1)} %bitcast.38), calls=%async_computation.1 | async-start | bytes 1835008 | tf_op jit(solution)/shard_map/all_to_all | solution.py:104
  50.0 12.8 %all-gather = f32[8,1,384]{2,1,0:T(1,128)S(1)} all-gather(f32[1,1,384]{2,1,0:T(1,128)S(1)} %reshape.100), channel_id=1, replica_groups=mesh['ep_x'=4,'ep_z'=8,'tp_y'=4,'tp_c'=2] {'tp_y','tp_c'}, dimensions={0}, use_global_device_ids=true | all-gather | bytes 13824 | tf_op jit(solution)/shard_map/all_gather | solution.py:458
  64.5 1.3 collective-permute-start.2
  65.8 2.0 collective-permute-start.4
  67.7 6.6 %all-to-all-done.1 = bf16[16,32,896]{2,0,1:T(8,128)(2,1)} async-done(((bf16[16,32,896]{2,0,1:T(8,128)(2,1)}), bf16[16,32,896]{2,0,1:T(8,128)(2,1)}, u32[]{:S(2)}, u32[]{:S(2)}) %all-to-all-start.1) | async-done | bytes 917536 | tf_op jit(solution)/shard_map/all_to_all | solution.py:104
  74.3 1.2 slice.76.refs_0_.refs_5_
  75.5 1.6 collective-permute-start.14
  77.2 9.1 %collective-permute-done.2.refs_2_.refs_4_ = bf16[512,768]{1,0:T(8,128)(2,1)S(1)} collective-permute-done((bf16[512,768]{1,0:T(8,128)(2,1)}, bf16[512,768]{1,0:T(8,128)(2,1)S(1)}, u32[]{:S(2)}, u32[]{:S(2)}) %collective-permute-start.2) | collective-permute-done | bytes 786464 | tf_op jit(solution)/shard_map/ppermute | solution.py:96
  87.3 1.8 collective-permute-start.3
  89.1 1.8 slice.73
  90.9 1.4 collective-permute-start.5
  92.6 8.3 %shard_map.147 = (f32[512,512]{1,0:T(8,128)}, f32[512,512]{1,0:T(8,128)}) custom-call(s32[2]{0:T(128)} %pad_add_fusion.at_ref.y_ref, bf16[512,768]{1,0:T(8,128)(2,1)} %bitcast.7.refs_0_, bf16[512,768]{1,0:T(8,128)(2,1)} %collective-permute-done.4.refs_1_, bf16[512,768]{1,0:T(8,128)(2,1)} %copy-done.13, bf16[256,3072]{1,0:T(8,128)(2,1)} %refs_0_.3, ...), custom_call_target="tpu_custom_call" | custom-call | flops 2415919104 | bytes 20000000 | tf_op jit(solution)/shard_map/pallas_call | solution.py:371
  101.0 2.2 collective-permute-done.14.refs_4_.refs_9_
  104.1 2.7 collective-permute-done.13.refs_1_.refs_6_
  107.6 1.2 collective-permute-start.16
  108.8 2.8 %collective-permute-done.3.refs_0_.refs_2_ = bf16[256,768]{1,0:T(8,128)(2,1)S(1)} collective-permute-done((bf16[256,768]{1,0:T(8,128)(2,1)}, bf16[256,768]{1,0:T(8,128)(2,1)S(1)}, u32[]{:S(2)}, u32[]{:S(2)}) %collective-permute-start.3) | collective-permute-done | bytes 393248 | tf_op jit(solution)/shard_map/ppermute | solution.py:96
  111.6 3.7 %collective-permute-done.5.refs_1_.refs_3_ = bf16[256,768]{1,0:T(8,128)(2,1)} collective-permute-done((bf16[256,768]{1,0:T(8,128)(2,1)}, bf16[256,768]{1,0:T(8,128)(2,1)}, u32[]{:S(2)}, u32[]{:S(2)}) %collective-permute-start.5) | collective-permute-done | bytes 393248 | tf_op jit(solution)/shard_map/ppermute | solution.py:96
  115.3 6.6 %shard_map.148 = (f32[512,512]{1,0:T(8,128)}, f32[512,512]{1,0:T(8,128)}, bf16[512,512]{1,0:T(8,128)(2,1)}, f32[32,128]{1,0:T(8,128)}) custom-call(s32[2]{0:T(128)} %pad_add_fusion.at_ref.y_ref, bf16[256,768]{1,0:T(8,128)(2,1)} %copy-done.12, bf16[256,768]{1,0:T(8,128)(2,1)} %collective-permute-done.5.refs_1_.refs_3_, bf16[256,3072]{1,0:T(8,128)(2,1)} %refs_0_.3, ...), custom_call_target="tpu_custom_call" | custom-call | flops 805306368 | bytes 20000000 | tf_op jit(solution)/shard_map/pallas_call | solution.py:371
  123.6 11.0 %all-to-all-start.3 = ((f32[2,256,32]{2,0,1:T(2,128)}), f32[2,256,32]{2,0,1:T(2,128)S(1)}, u32[]{:S(2)}, u32[]{:S(2)}) async-start(f32[2,256,32]{2,0,1:T(2,128)} %broadcast_in_dim.36), calls=%async_computation.3 | async-start | bytes 524288 | tf_op jit(solution)/shard_map/all_to_all | solution.py:505
  134.6 3.4 %shard_map.150 = (bf16[256,768]{1,0:T(8,128)(2,1)}, bf16[256,768]{1,0:T(8,128)(2,1)}) custom-call(s32[2]{0:T(128)} %pad_add_fusion.at_ref.y_ref, bf16[512,512]{1,0:T(8,128)(2,1)} %get-tuple-element.44.hidden_ref.refs_10_, bf16[256,3072]{1,0:T(8,128)(2,1)} %refs_5_.3, bf16[256,3072]{1,0:T(8,128)(2,1)} %copy-done.1), custom_call_target="tpu_custom_call" | custom-call | flops 402653184 | bytes 20000000 | tf_op jit(solution)/shard_map/pallas_call | solution.py:371
  137.9 2.9 %collective-permute-start.10 = (bf16[256,768]{1,0:T(8,128)(2,1)}, bf16[256,768]{1,0:T(8,128)(2,1)S(1)}, u32[]{:S(2)}, u32[]{:S(2)}) collective-permute-start(bf16[256,768]{1,0:T(8,128)(2,1)} %get-tuple-element.49), channel_id=1, source_target_pairs={{0,6},{2,0},{4,2},{6,4},{1,7},{3,1},{5,3},{7,5},{8,14},{10,8},{12,... | collective-permute-start | bytes 1179656 | tf_op jit(solution)/shard_map/ppermute | solution.py:96
  140.8 5.8 %shard_map.149 = (bf16[512,768]{1,0:T(8,128)(2,1)}, bf16[512,768]{1,0:T(8,128)(2,1)}, bf16[512,768]{1,0:T(8,128)(2,1)}) custom-call(s32[2]{0:T(128)} %pad_add_fusion.at_ref.y_ref, bf16[512,512]{1,0:T(8,128)(2,1)} %get-tuple-element.44.hidden_ref.refs_10_, bf16[256,3072]{1,0:T(8,128)(2,1)} %refs_5_.3, bf16[256,3072]{1,0:T(8,128)(2,1)} %copy-done.1), custom_call_target="tpu_custom_call" | custom-call | flops 1207959552 | bytes 20000000 | tf_op jit(solution)/shard_map/pallas_call | solution.py:371
  146.6 2.4 all-to-all-done.3
  151.1 1.2 add_convert_fusion.7
  152.3 3.3 %collective-permute-start.11 = (bf16[512,768]{1,0:T(8,128)(2,1)S(1)}, bf16[512,768]{1,0:T(8,128)(2,1)S(1)}, u32[]{:S(2)}, u32[]{:S(2)}) collective-permute-start(bf16[512,768]{1,0:T(8,128)(2,1)S(1)} %add_convert_fusion.7), channel_id=1, source_target_pairs={{0,6},{2,0},{4,2},{6,4},{1,7},{3,1},{5,3},{7,5},{8,14},{10,8},{12,... | collective-permute-start | bytes 2359304 | tf_op jit(solution)/shard_map/ppermute | solution.py:96
  155.6 1.0 add_convert_fusion.8
  156.7 7.1 %shard_map.151.refs_7_ = f32[512,512]{1,0:T(8,128)} custom-call(s32[2]{0:T(128)} %pad_add_fusion.at_ref.y_ref, bf16[512,768]{1,0:T(8,128)(2,1)} %copy-done.2, bf16[512,768]{1,0:T(8,128)(2,1)} %copy-done.4, bf16[256,768]{1,0:T(8,128)(2,1)} %collective-permute-done.15.refs_2_.refs_7_, bf16[256,768]{1,0:T(8,128)(2,1)} %collective-permute-done.16.refs_3_.refs_8_, ...), custom_call_target="tpu_custom_call" | custom-call | flops 1610612736 | bytes 20000000 | tf_op jit(solution)/shard_map/pallas_call | solution.py:371
  163.7 5.9 %shard_map.152 = (bf16[512,512]{1,0:T(8,128)(2,1)}, bf16[512,512]{1,0:T(8,128)(2,1)}, f32[512,1]{1,0:T(8,128)}, bf16[256,768]{1,0:T(8,128)(2,1)}, bf16[256,768]{1,0:T(8,128)(2,1)}) custom-call(s32[2]{0:T(128)} %pad_add_fusion.at_ref.y_ref, bf16[256,3072]{1,0:T(8,128)(2,1)} %refs_0_.3, bf16[256,3072]{1,0:T(8,128)(2,1)} %collective-permute-done.6.refs_4_.refs_3_.refs_1_, ...), custom_call_target="tpu_custom_call" | custom-call | flops 805306368 | bytes 20000000 | tf_op jit(solution)/shard_map/pallas_call | solution.py:371
  169.6 3.2 %collective-permute-start.19 = (bf16[256,768]{1,0:T(8,128)(2,1)}, bf16[256,768]{1,0:T(8,128)(2,1)}, u32[]{:S(2)}, u32[]{:S(2)}) collective-permute-start(bf16[256,768]{1,0:T(8,128)(2,1)} %get-tuple-element.61), channel_id=1, source_target_pairs={{0,6},{2,0},{4,2},{6,4},{1,7},{3,1},{5,3},{7,5},{8,14},{10,8},{12,... | collective-permute-start | bytes 1179656 | tf_op jit(solution)/shard_map/ppermute | solution.py:96
  172.8 14.9 %shard_map.154 = (bf16[768,3072]{1,0:T(8,128)(2,1)}, bf16[768,3072]{1,0:T(8,128)(2,1)}) custom-call(s32[2]{0:T(128)} %pad_add_fusion.at_ref.y_ref, bf16[512,768]{1,0:T(8,128)(2,1)} %bitcast.7.refs_0_, bf16[512,768]{1,0:T(8,128)(2,1)} %collective-permute-done.4.refs_1_, bf16[256,768]{1,0:T(8,128)(2,1)} %copy-done.12, ...), custom_call_target="tpu_custom_call" | custom-call | flops 4831838208 | bytes 20000000 | tf_op jit(solution)/shard_map/pallas_call | solution.py:371
  187.8 7.5 %shard_map.153 = (bf16[512,768]{1,0:T(8,128)(2,1)}, bf16[512,768]{1,0:T(8,128)(2,1)}, bf16[512,768]{1,0:T(8,128)(2,1)}) custom-call(s32[2]{0:T(128)} %pad_add_fusion.at_ref.y_ref, bf16[256,3072]{1,0:T(8,128)(2,1)} %refs_0_.3, bf16[256,3072]{1,0:T(8,128)(2,1)} %collective-permute-done.6.refs_4_.refs_3_.refs_1_, bf16[256,3072]{1,0:T(8,128)(2,1)} %refs_2_.5, ...), custom_call_target="tpu_custom_call" | custom-call | flops 2415919104 | bytes 20000000 | tf_op jit(solution)/shard_map/pallas_call | solution.py:371
  195.4 1.2 add_convert_fusion.6
  196.5 9.8 %all-to-all-start.2 = ((bf16[16,32,768]{2,0,1:T(8,128)(2,1)}), bf16[16,32,768]{2,0,1:T(8,128)(2,1)S(1)}, u32[]{:S(2)}, u32[]{:S(2)}) async-start(bf16[16,32,768]{2,0,1:T(8,128)(2,1)} %bitcast.15), calls=%async_computation.2 | async-start | bytes 1572864 | tf_op jit(solution)/shard_map/all_to_all | solution.py:104
  206.4 1.2 add_convert_fusion.4
  207.5 3.1 %collective-permute-start.20 = (bf16[512,768]{1,0:T(8,128)(2,1)S(1)}, bf16[512,768]{1,0:T(8,128)(2,1)S(1)}, u32[]{:S(2)}, u32[]{:S(2)}) collective-permute-start(bf16[512,768]{1,0:T(8,128)(2,1)S(1)} %add_convert_fusion.4), channel_id=1, source_target_pairs={{0,6},{2,0},{4,2},{6,4},{1,7},{3,1},{5,3},{7,5},{8,14},{10,8},{12,... | collective-permute-start | bytes 2359304 | tf_op jit(solution)/shard_map/ppermute | solution.py:96
  210.6 1.1 add_convert_fusion.5
  211.8 15.6 %collective-permute-done.20 = bf16[512,768]{1,0:T(8,128)(2,1)S(1)} collective-permute-done((bf16[512,768]{1,0:T(8,128)(2,1)S(1)}, bf16[512,768]{1,0:T(8,128)(2,1)S(1)}, u32[]{:S(2)}, u32[]{:S(2)}) %collective-permute-start.20) | collective-permute-done | bytes 786464 | tf_op jit(solution)/shard_map/ppermute | solution.py:96
  227.3 4.6 %collective-permute-done.18 = bf16[512,768]{1,0:T(8,128)(2,1)S(1)} collective-permute-done((bf16[512,768]{1,0:T(8,128)(2,1)S(1)}, bf16[512,768]{1,0:T(8,128)(2,1)S(1)}, u32[]{:S(2)}, u32[]{:S(2)}) %collective-permute-start.18) | collective-permute-done | bytes 786464 | tf_op jit(solution)/shard_map/ppermute | solution.py:96
  232.0 1.2 add_convert_fusion.3
  233.1 9.8 %all-to-all-start.4 = ((bf16[16,32,768]{2,0,1:T(8,128)(2,1)}), bf16[16,32,768]{2,0,1:T(8,128)(2,1)S(1)}, u32[]{:S(2)}, u32[]{:S(2)}) async-start(bf16[16,32,768]{2,0,1:T(8,128)(2,1)} %bitcast.21), calls=%async_computation.4 | async-start | bytes 1572864 | tf_op jit(solution)/shard_map/all_to_all | solution.py:104
  244.5 20.4 %all-to-all-done.4 = bf16[16,32,768]{2,0,1:T(8,128)(2,1)S(1)} async-done(((bf16[16,32,768]{2,0,1:T(8,128)(2,1)}), bf16[16,32,768]{2,0,1:T(8,128)(2,1)S(1)}, u32[]{:S(2)}, u32[]{:S(2)}) %all-to-all-start.4) | async-done | bytes 786464 | tf_op jit(solution)/shard_map/all_to_all | solution.py:104
  267.3 5.9 %add_convert_fusion = (bf16[256,3072]{1,0:T(8,128)(2,1)}, bf16[256,3072]{1,0:T(8,128)(2,1)}, bf16[256,3072]{1,0:T(8,128)(2,1)}) fusion(bf16[768,3072]{1,0:T(8,128)(2,1)} %collective-permute-done.22, bf16[768,3072]{1,0:T(8,128)(2,1)} %get-tuple-element.63), kind=kLoop, calls=%fused_computation | loop fusion | flops 9437184 | bytes 14155776 | tf_op jit(solution)/shard_map/convert_element_type | solution.py:118
  (108 shorter events, 14.5 us)
Async XLA Ops:
  0.6 19.7 %copy-start = (bf16[256,3072]{1,0:T(8,128)(2,1)S(1)}, bf16[256,3072]{1,0:T(8,128)(2,1)}, u32[]{:S(2)}) copy-start(bf16[256,3072]{1,0:T(8,128)(2,1)} %refs_5_.3) | copy-start | bytes 4718596
  4.1 1.7 collective-permute-start
  9.1 34.6 %all-to-all-start = ((bf16[16,32,768]{2,0,1:T(8,128)(2,1)}), bf16[16,32,768]{2,0,1:T(8,128)(2,1)}, u32[]{:S(2)}, u32[]{:S(2)}) async-start(bf16[16,32,768]{2,0,1:T(8,128)(2,1)} %bitcast.39), calls=%async_computation | async-start | bytes 1572864 | tf_op jit(solution)/shard_map/all_to_all | solution.py:104
  20.3 42.4 %collective-permute-start.1 = (bf16[256,3072]{1,0:T(8,128)(2,1)S(1)}, bf16[256,3072]{1,0:T(8,128)(2,1)S(1)}, u32[]{:S(2)}, u32[]{:S(2)}) collective-permute-start(bf16[256,3072]{1,0:T(8,128)(2,1)S(1)} %copy-done), channel_id=1, source_target_pairs={{0,1},{1,0},{2,3},{3,2},{4,5},{5,4},{6,7},{7,6},{8,9},{9,8},{10,11... | collective-permute-start | bytes 4718600 | tf_op jit(solution)/shard_map/ppermute | solution.py:100
  20.4 29.0 %copy-start.17 = (f32[384]{0:T(512)S(1)}, f32[384]{0:T(512)}, u32[]{:S(2)}) copy-start(f32[384]{0:T(512)} %param.15) | copy-start | bytes 4612
  20.4 29.0 %copy-start.5 = (bf16[128,384]{1,0:T(8,128)(2,1)S(1)}, bf16[128,384]{1,0:T(8,128)(2,1)}, u32[]{:S(2)}) copy-start(bf16[128,384]{1,0:T(8,128)(2,1)} %tokens_ref.1) | copy-start | bytes 294916
  43.6 30.7 %all-to-all-start.1 = ((bf16[16,32,896]{2,0,1:T(8,128)(2,1)}), bf16[16,32,896]{2,0,1:T(8,128)(2,1)}, u32[]{:S(2)}, u32[]{:S(2)}) async-start(bf16[16,32,896]{2,0,1:T(8,128)(2,1)} %bitcast.38), calls=%async_computation.1 | async-start | bytes 1835008 | tf_op jit(solution)/shard_map/all_to_all | solution.py:104
  48.8 42.1 %collective-permute-start.6 = (bf16[256,3072]{1,0:T(8,128)(2,1)}, bf16[256,3072]{1,0:T(8,128)(2,1)}, u32[]{:S(2)}, u32[]{:S(2)}) collective-permute-start(bf16[256,3072]{1,0:T(8,128)(2,1)} %refs_0_.3), channel_id=1, source_target_pairs={{0,1},{1,0},{2,3},{3,2},{4,5},{5,4},{6,7},{7,6},{8,9},{9,8},{10,11... | collective-permute-start | bytes 4718600 | tf_op jit(solution)/shard_map/ppermute | solution.py:100
  48.9 43.7 %collective-permute-start.7 = (bf16[256,3072]{1,0:T(8,128)(2,1)}, bf16[256,3072]{1,0:T(8,128)(2,1)}, u32[]{:S(2)}, u32[]{:S(2)}) collective-permute-start(bf16[256,3072]{1,0:T(8,128)(2,1)} %refs_2_.5), channel_id=1, source_target_pairs={{0,1},{1,0},{2,3},{3,2},{4,5},{5,4},{6,7},{7,6},{8,9},{9,8},{10,11... | collective-permute-start | bytes 4718600 | tf_op jit(solution)/shard_map/ppermute | solution.py:100
  62.8 0.7 copy-start.16
  62.8 1.1 copy-start.1
  64.5 21.8 %collective-permute-start.2 = (bf16[512,768]{1,0:T(8,128)(2,1)}, bf16[512,768]{1,0:T(8,128)(2,1)S(1)}, u32[]{:S(2)}, u32[]{:S(2)}) collective-permute-start(bf16[512,768]{1,0:T(8,128)(2,1)} %bitcast.7.refs_0_), channel_id=1, source_target_pairs={{0,2},{2,4},{4,6},{6,0},{1,3},{3,5},{5,7},{7,1},{8,10},{10,12},{12... | collective-permute-start | bytes 2359304 | tf_op jit(solution)/shard_map/ppermute | solution.py:96
  65.8 21.6 %collective-permute-start.4 = (bf16[512,768]{1,0:T(8,128)(2,1)}, bf16[512,768]{1,0:T(8,128)(2,1)}, u32[]{:S(2)}, u32[]{:S(2)}) collective-permute-start(bf16[512,768]{1,0:T(8,128)(2,1)} %bitcast.7.refs_0_), channel_id=1, source_target_pairs={{0,6},{2,0},{4,2},{6,4},{1,7},{3,1},{5,3},{7,5},{8,14},{10,8},{12,... | collective-permute-start | bytes 2359304 | tf_op jit(solution)/shard_map/ppermute | solution.py:96
  74.3 18.0 %copy-start.20 = (s32[64]{0:T(128)S(1)}, s32[64]{0:T(128)}, u32[]{:S(2)}) copy-start(s32[64]{0:T(128)} %param.17) | copy-start | bytes 772
  75.5 25.4 %copy-start.2 = (bf16[512,768]{1,0:T(8,128)(2,1)}, bf16[512,768]{1,0:T(8,128)(2,1)S(1)}, u32[]{:S(2)}) copy-start(bf16[512,768]{1,0:T(8,128)(2,1)S(1)} %slice.76.refs_0_.refs_5_) | copy-start | bytes 2359300
  75.5 27.6 %collective-permute-start.14 = (bf16[512,768]{1,0:T(8,128)(2,1)S(1)}, bf16[512,768]{1,0:T(8,128)(2,1)S(1)}, u32[]{:S(2)}, u32[]{:S(2)}) collective-permute-start(bf16[512,768]{1,0:T(8,128)(2,1)S(1)} %slice.76.refs_0_.refs_5_), channel_id=1, source_target_pairs={{0,2},{2,4},{4,6},{6,0},{1,3},{3,5},{5,7},{7,1},{8,10},{10,12},{12... | collective-permute-start | bytes 2359304 | tf_op jit(solution)/shard_map/ppermute | solution.py:96
  86.3 1.0 copy-start.13
  86.3 20.4 %collective-permute-start.13 = (bf16[512,768]{1,0:T(8,128)(2,1)S(1)}, bf16[512,768]{1,0:T(8,128)(2,1)S(1)}, u32[]{:S(2)}, u32[]{:S(2)}) collective-permute-start(bf16[512,768]{1,0:T(8,128)(2,1)S(1)} %slice.76.refs_0_.refs_5_), channel_id=1, source_target_pairs={{0,6},{2,0},{4,2},{6,4},{1,7},{3,1},{5,3},{7,5},{8,14},{10,8},{12,... | collective-permute-start | bytes 2359304 | tf_op jit(solution)/shard_map/ppermute | solution.py:96
  87.3 24.3 %collective-permute-start.3 = (bf16[256,768]{1,0:T(8,128)(2,1)}, bf16[256,768]{1,0:T(8,128)(2,1)S(1)}, u32[]{:S(2)}, u32[]{:S(2)}) collective-permute-start(bf16[256,768]{1,0:T(8,128)(2,1)} %slice.72), channel_id=1, source_target_pairs={{0,2},{2,4},{4,6},{6,0},{1,3},{3,5},{5,7},{7,1},{8,10},{10,12},{12... | collective-permute-start | bytes 1179656 | tf_op jit(solution)/shard_map/ppermute | solution.py:96
  90.9 24.4 %collective-permute-start.5 = (bf16[256,768]{1,0:T(8,128)(2,1)}, bf16[256,768]{1,0:T(8,128)(2,1)}, u32[]{:S(2)}, u32[]{:S(2)}) collective-permute-start(bf16[256,768]{1,0:T(8,128)(2,1)} %slice.73), channel_id=1, source_target_pairs={{0,6},{2,0},{4,2},{6,4},{1,7},{3,1},{5,3},{7,5},{8,14},{10,8},{12,... | collective-permute-start | bytes 1179656 | tf_op jit(solution)/shard_map/ppermute | solution.py:96
  103.2 18.7 %copy-start.3 = (bf16[512,768]{1,0:T(8,128)(2,1)}, bf16[512,768]{1,0:T(8,128)(2,1)S(1)}, u32[]{:S(2)}) copy-start(bf16[512,768]{1,0:T(8,128)(2,1)S(1)} %collective-permute-done.14.refs_4_.refs_9_) | copy-start | bytes 2359300
  104.0 52.7 %collective-permute-start.15 = (bf16[256,768]{1,0:T(8,128)(2,1)}, bf16[256,768]{1,0:T(8,128)(2,1)}, u32[]{:S(2)}, u32[]{:S(2)}) collective-permute-start(bf16[256,768]{1,0:T(8,128)(2,1)} %slice.77), channel_id=1, source_target_pairs={{0,2},{2,4},{4,6},{6,0},{1,3},{3,5},{5,7},{7,1},{8,10},{10,12},{12... | collective-permute-start | bytes 1179656 | tf_op jit(solution)/shard_map/ppermute | solution.py:96
  106.7 15.1 %copy-start.4 = (bf16[512,768]{1,0:T(8,128)(2,1)}, bf16[512,768]{1,0:T(8,128)(2,1)S(1)}, u32[]{:S(2)}) copy-start(bf16[512,768]{1,0:T(8,128)(2,1)S(1)} %collective-permute-done.13.refs_1_.refs_6_) | copy-start | bytes 2359300
  107.6 49.1 %collective-permute-start.16 = (bf16[256,768]{1,0:T(8,128)(2,1)}, bf16[256,768]{1,0:T(8,128)(2,1)}, u32[]{:S(2)}, u32[]{:S(2)}) collective-permute-start(bf16[256,768]{1,0:T(8,128)(2,1)} %slice.78), channel_id=1, source_target_pairs={{0,6},{2,0},{4,2},{6,4},{1,7},{3,1},{5,3},{7,5},{8,14},{10,8},{12,... | collective-permute-start | bytes 1179656 | tf_op jit(solution)/shard_map/ppermute | solution.py:96
  111.6 3.7 %copy-start.12 = (bf16[256,768]{1,0:T(8,128)(2,1)}, bf16[256,768]{1,0:T(8,128)(2,1)S(1)}, u32[]{:S(2)}) copy-start(bf16[256,768]{1,0:T(8,128)(2,1)S(1)} %collective-permute-done.3.refs_0_.refs_2_) | copy-start | bytes 1179652
  123.6 25.5 %all-to-all-start.3 = ((f32[2,256,32]{2,0,1:T(2,128)}), f32[2,256,32]{2,0,1:T(2,128)S(1)}, u32[]{:S(2)}, u32[]{:S(2)}) async-start(f32[2,256,32]{2,0,1:T(2,128)} %broadcast_in_dim.36), calls=%async_computation.3 | async-start | bytes 524288 | tf_op jit(solution)/shard_map/all_to_all | solution.py:505
  137.9 13.2 %collective-permute-start.10 = (bf16[256,768]{1,0:T(8,128)(2,1)}, bf16[256,768]{1,0:T(8,128)(2,1)S(1)}, u32[]{:S(2)}, u32[]{:S(2)}) collective-permute-start(bf16[256,768]{1,0:T(8,128)(2,1)} %get-tuple-element.49), channel_id=1, source_target_pairs={{0,6},{2,0},{4,2},{6,4},{1,7},{3,1},{5,3},{7,5},{8,14},{10,8},{12,... | collective-permute-start | bytes 1179656 | tf_op jit(solution)/shard_map/ppermute | solution.py:96
  140.8 14.8 %collective-permute-start.8 = (bf16[256,768]{1,0:T(8,128)(2,1)}, bf16[256,768]{1,0:T(8,128)(2,1)S(1)}, u32[]{:S(2)}, u32[]{:S(2)}) collective-permute-start(bf16[256,768]{1,0:T(8,128)(2,1)} %get-tuple-element.47), channel_id=1, source_target_pairs={{0,2},{2,4},{4,6},{6,0},{1,3},{3,5},{5,7},{7,1},{8,10},{10,12},{12... | collective-permute-start | bytes 1179656 | tf_op jit(solution)/shard_map/ppermute | solution.py:96
  146.6 9.0 %copy-start.8 = (bf16[512,768]{1,0:T(8,128)(2,1)S(1)}, bf16[512,768]{1,0:T(8,128)(2,1)}, u32[]{:S(2)}) copy-start(bf16[512,768]{1,0:T(8,128)(2,1)} %get-tuple-element.46) | copy-start | bytes 2359300
  149.4 7.3 %copy-start.18 = (f32[64]{0:T(128)}, f32[64]{0:T(128)S(1)}, u32[]{:S(2)}) copy-start(f32[64]{0:T(128)S(1)} %div.26) | copy-start | bytes 772
  152.3 43.0 %collective-permute-start.11 = (bf16[512,768]{1,0:T(8,128)(2,1)S(1)}, bf16[512,768]{1,0:T(8,128)(2,1)S(1)}, u32[]{:S(2)}, u32[]{:S(2)}) collective-permute-start(bf16[512,768]{1,0:T(8,128)(2,1)S(1)} %add_convert_fusion.7), channel_id=1, source_target_pairs={{0,6},{2,0},{4,2},{6,4},{1,7},{3,1},{5,3},{7,5},{8,14},{10,8},{12,... | collective-permute-start | bytes 2359304 | tf_op jit(solution)/shard_map/ppermute | solution.py:96
  156.7 38.7 %collective-permute-start.9 = (bf16[512,768]{1,0:T(8,128)(2,1)}, bf16[512,768]{1,0:T(8,128)(2,1)S(1)}, u32[]{:S(2)}, u32[]{:S(2)}) collective-permute-start(bf16[512,768]{1,0:T(8,128)(2,1)} %add_convert_fusion.8), channel_id=1, source_target_pairs={{0,2},{2,4},{4,6},{6,0},{1,3},{3,5},{5,7},{7,1},{8,10},{10,12},{12... | collective-permute-start | bytes 2359304 | tf_op jit(solution)/shard_map/ppermute | solution.py:96
  169.6 36.7 %collective-permute-start.19 = (bf16[256,768]{1,0:T(8,128)(2,1)}, bf16[256,768]{1,0:T(8,128)(2,1)}, u32[]{:S(2)}, u32[]{:S(2)}) collective-permute-start(bf16[256,768]{1,0:T(8,128)(2,1)} %get-tuple-element.61), channel_id=1, source_target_pairs={{0,6},{2,0},{4,2},{6,4},{1,7},{3,1},{5,3},{7,5},{8,14},{10,8},{12,... | collective-permute-start | bytes 1179656 | tf_op jit(solution)/shard_map/ppermute | solution.py:96
  172.8 37.8 %collective-permute-start.17 = (bf16[256,768]{1,0:T(8,128)(2,1)}, bf16[256,768]{1,0:T(8,128)(2,1)}, u32[]{:S(2)}, u32[]{:S(2)}) collective-permute-start(bf16[256,768]{1,0:T(8,128)(2,1)} %get-tuple-element.59), channel_id=1, source_target_pairs={{0,2},{2,4},{4,6},{6,0},{1,3},{3,5},{5,7},{7,1},{8,10},{10,12},{12... | collective-permute-start | bytes 1179656 | tf_op jit(solution)/shard_map/ppermute | solution.py:96
  187.7 7.7 %copy-start.6 = (bf16[512,768]{1,0:T(8,128)(2,1)S(1)}, bf16[512,768]{1,0:T(8,128)(2,1)}, u32[]{:S(2)}) copy-start(bf16[512,768]{1,0:T(8,128)(2,1)} %get-tuple-element.45) | copy-start | bytes 2359300
  187.7 79.6 %collective-permute-start.22 = (bf16[768,3072]{1,0:T(8,128)(2,1)}, bf16[768,3072]{1,0:T(8,128)(2,1)}, u32[]{:S(2)}, u32[]{:S(2)}) collective-permute-start(bf16[768,3072]{1,0:T(8,128)(2,1)} %get-tuple-element.64), channel_id=1, source_target_pairs={{0,1},{1,0},{2,3},{3,2},{4,5},{5,4},{6,7},{7,6},{8,9},{9,8},{10,11... | collective-permute-start | bytes 14155784 | tf_op jit(solution)/shard_map/ppermute | solution.py:100
  196.5 9.8 %copy-start.10 = (bf16[512,768]{1,0:T(8,128)(2,1)S(1)}, bf16[512,768]{1,0:T(8,128)(2,1)}, u32[]{:S(2)}) copy-start(bf16[512,768]{1,0:T(8,128)(2,1)} %get-tuple-element.60) | copy-start | bytes 2359300
  196.5 14.1 %copy-start.9 = (bf16[512,768]{1,0:T(8,128)(2,1)S(1)}, bf16[512,768]{1,0:T(8,128)(2,1)}, u32[]{:S(2)}) copy-start(bf16[512,768]{1,0:T(8,128)(2,1)} %get-tuple-element.58) | copy-start | bytes 2359300
  196.5 36.6 %all-to-all-start.2 = ((bf16[16,32,768]{2,0,1:T(8,128)(2,1)}), bf16[16,32,768]{2,0,1:T(8,128)(2,1)S(1)}, u32[]{:S(2)}, u32[]{:S(2)}) async-start(bf16[16,32,768]{2,0,1:T(8,128)(2,1)} %bitcast.15), calls=%async_computation.2 | async-start | bytes 1572864 | tf_op jit(solution)/shard_map/all_to_all | solution.py:104
  206.3 25.6 %copy-start.7 = (bf16[512,768]{1,0:T(8,128)(2,1)S(1)}, bf16[512,768]{1,0:T(8,128)(2,1)}, u32[]{:S(2)}) copy-start(bf16[512,768]{1,0:T(8,128)(2,1)} %get-tuple-element.57) | copy-start | bytes 2359300
  207.5 19.8 %collective-permute-start.20 = (bf16[512,768]{1,0:T(8,128)(2,1)S(1)}, bf16[512,768]{1,0:T(8,128)(2,1)S(1)}, u32[]{:S(2)}, u32[]{:S(2)}) collective-permute-start(bf16[512,768]{1,0:T(8,128)(2,1)S(1)} %add_convert_fusion.4), channel_id=1, source_target_pairs={{0,6},{2,0},{4,2},{6,4},{1,7},{3,1},{5,3},{7,5},{8,14},{10,8},{12,... | collective-permute-start | bytes 2359304 | tf_op jit(solution)/shard_map/ppermute | solution.py:96
  211.7 20.2 %collective-permute-start.18 = (bf16[512,768]{1,0:T(8,128)(2,1)S(1)}, bf16[512,768]{1,0:T(8,128)(2,1)S(1)}, u32[]{:S(2)}, u32[]{:S(2)}) collective-permute-start(bf16[512,768]{1,0:T(8,128)(2,1)S(1)} %add_convert_fusion.5), channel_id=1, source_target_pairs={{0,2},{2,4},{4,6},{6,0},{1,3},{3,5},{5,7},{7,1},{8,10},{10,12},{12... | collective-permute-start | bytes 2359304 | tf_op jit(solution)/shard_map/ppermute | solution.py:96
  233.1 31.8 %all-to-all-start.4 = ((bf16[16,32,768]{2,0,1:T(8,128)(2,1)}), bf16[16,32,768]{2,0,1:T(8,128)(2,1)S(1)}, u32[]{:S(2)}, u32[]{:S(2)}) async-start(bf16[16,32,768]{2,0,1:T(8,128)(2,1)} %bitcast.21), calls=%async_computation.4 | async-start | bytes 1572864 | tf_op jit(solution)/shard_map/all_to_all | solution.py:104
  242.9 22.2 %copy-start.14 = (f32[256,128]{1,0:T(8,128)S(1)}, f32[256,128]{1,0:T(8,128)}, u32[]{:S(2)}) copy-start(f32[256,128]{1,0:T(8,128)} %get-tuple-element.36) | copy-start | bytes 393220
  243.0 23.4 %copy-start.15 = (bf16[128,384]{1,0:T(8,128)(2,1)S(1)}, bf16[128,384]{1,0:T(8,128)(2,1)}, u32[]{:S(2)}) copy-start(bf16[128,384]{1,0:T(8,128)(2,1)} %upstream_ref.1) | copy-start | bytes 294916
  243.0 23.4 %copy-start.19 = (bf16[256,128]{1,0:T(8,128)(2,1)S(1)}, bf16[256,128]{1,0:T(8,128)(2,1)}, u32[]{:S(2)}) copy-start(bf16[256,128]{1,0:T(8,128)(2,1)} %get-tuple-element.52) | copy-start | bytes 196612
  243.1 1.4 collective-permute-start.12
  265.0 1.4 collective-permute-start.21
  (1 other events, 0.7 us)
